TPU v7x, 32 devices: a whole 2x2x4 slice. The times are simulated.
32 devices in a mesh: between: 4 (over y, core), inside: 8 (over z, x).
Axes of the slice: x: 2, y: 2, z: 4, core: 2. Of those that a mesh axis runs over, the one named last changes fastest.
Arguments:
- inputs: bfloat16 [16384, 4096], P(('between', 'inside')), may hold values from -6 to 6
- grad_out: bfloat16 [16384, 1024], P(('between', 'inside')), may hold values from -6 to 6
- error: float32 [4, 4096, 1024], P('between', 'inside'), may hold values from -4 to 4
- momentum: float32 [4096, 1024], P('inside'), may hold values from -4 to 4
- weight: bfloat16 [4096, 1024], P('inside'), may hold values from -6 to 6
- tile_index: int32 [4, 8, 4, 32], P('between', 'inside'), may hold values from -1 to 1023, as said below
Outputs:
- new_weight: bfloat16 [4096, 1024], replicated
- new_momentum: float32 [4096, 1024], P('inside')
- new_error: float32 [4, 4096, 1024], P('between', 'inside')
Inputs may be any that keep to these rules, and one draw needn't show every extreme that they name: `tile_index`: for each island, device and owning island the live entries are distinct and stand first, the rest are -1; their number varies strongly from block to block, and in every draw some device and owner have all 32 slots live on all 4 islands.
All inputs are finite; a program needn't handle non-finite values.
Results may differ from a plain program's by a relative error of at most 0.0035.
Values may be sent and summed in bfloat16 or wider, within the bound.
No kernel may reach another device: no remote copies, remote signals or barrier semaphores. Data moves between devices by JAX's collectives and lax.ppermute only.
A program may use at most 128 MiB of HBM per device.

v0:
```python
import math

import jax
import jax.numpy as jnp
from jax import lax
from jax.sharding import PartitionSpec as P

TILE = 128


feedback_decay = 0.95
outer_rate = 0.7
outer_momentum = 0.9


def tile_sum(values, places, own_tiles):
    onehot = (places[:, :, None] == jnp.arange(own_tiles, dtype=jnp.int32)).astype(jnp.bfloat16)
    return lax.dot_general(
        onehot, values, (((0, 1), (0, 1)), ((), ())), preferred_element_type=jnp.float32
    )


def outer_step(delta, momentum_rows, weight_rows):
    moment = outer_momentum * momentum_rows + delta
    updated = weight_rows.astype(jnp.float32) - outer_rate * (delta + outer_momentum * moment)
    return (updated.astype(jnp.bfloat16), moment)


def local(inputs, grad_out, error, momentum, weight, tile_index):
    group = lax.axis_size("inside")
    islands = lax.axis_size("between")
    feat = inputs.shape[1]
    width = grad_out.shape[1]
    rows_dev = feat // group
    own_rows = rows_dev // islands
    tiles_row = width // TILE
    own_tiles = own_rows * tiles_row
    grad = lax.psum_scatter(
        lax.dot_general(
            inputs, grad_out, (((0,), (0,)), ((), ())), preferred_element_type=jnp.float32
        ),
        "inside",
        scatter_dimension=0,
        tiled=True,
    )
    scale = 1.0 / math.sqrt(inputs.shape[0] * group)
    accum = feedback_decay * error[0] + scale * grad
    index = tile_index[0, 0]
    hit = jnp.any(index[:, :, None] == jnp.arange(own_tiles, dtype=jnp.int32), axis=1)
    tiles = accum.reshape(islands, own_tiles, TILE)
    new_error = jnp.where(hit[:, :, None], 0.0, tiles).reshape(1, rows_dev, width)
    picked = jnp.take_along_axis(tiles, jnp.maximum(index, 0)[:, :, None], axis=1)
    slots = jnp.where(index[:, :, None] >= 0, picked, 0.0).astype(jnp.bfloat16)
    start = lax.axis_index("between") * own_rows
    values, places = (
        lax.all_to_all(slots, "between", split_axis=0, concat_axis=0, tiled=True),
        lax.all_to_all(index, "between", split_axis=0, concat_axis=0, tiled=True),
    )
    delta = tile_sum(values, places, own_tiles).reshape(own_rows, width) / islands
    new_rows, new_moment = outer_step(
        delta,
        lax.dynamic_slice_in_dim(momentum, start, own_rows, 0),
        lax.dynamic_slice_in_dim(weight, start, own_rows, 0),
    )
    moment = lax.all_gather(new_moment, "between", axis=0, tiled=True)
    blocks = lax.all_gather(new_rows, ("between", "inside"), axis=0, tiled=True)
    whole = (
        blocks.reshape(islands, group, own_rows, width).transpose(1, 0, 2, 3).reshape(feat, width)
    )
    return (whole, moment, new_error)


def solution(mesh):
    in_specs = (
        P(("between", "inside"), None),
        P(("between", "inside"), None),
        P("between", "inside", None),
        P("inside", None),
        P("inside", None),
        P("between", "inside", None, None),
    )
    out_specs = (P(), P("inside", None), P("between", "inside", None))
    return jax.shard_map(local, mesh=mesh, in_specs=in_specs, out_specs=out_specs, check_vma=False)
```

profile of v0, /device:TPU:0, one launch (start us, length us, event | category | flops | bytes accessed | tf_op | source)
XLA Modules:
  0.0 436.3 jit_solution(15180391349051026678)
XLA Ops:
  7.2 0.0 copy-start
  7.2 0.0 reduce-scatter.2.cloned.1.call-start
  7.2 1.2 copy-done
  8.4 10.4 %fusion.3 = f32[4096,1024]{1,0:T(8,128)} fusion(bf16[512,4096]{1,0:T(8,128)(2,1)} %param.6, bf16[512,1024]{1,0:T(8,128)(2,1)S(1)} %copy-done), kind=kOutput, calls=%fused_computation.15 | convolution fusion | flops 4294967296 | bytes 22020096 | tf_op jit(solution)/shard_map/dot_general | solution.py:39
  18.7 0.0 reduce-scatter.2.cloned.1.call-update
  18.8 4.3 all-to-all-start
  23.0 0.9 fusion.1
  23.9 0.8 broadcast_in_dim.43
  24.7 0.6 broadcast_in_dim.44
  25.3 0.7 bitcast_or_fusion
  26.0 0.1 reshape.65
  26.1 0.7 broadcast_compare_fusion
  26.8 275.1 %reduce-scatter.2.cloned.1.call-done = f32[512,1024]{1,0:T(8,128)} async-done(((f32[4096,1024]{1,0:T(8,128)}), f32[512,1024]{1,0:T(8,128)}) %reduce-scatter.2.cloned.1.call-update) | async-done | bytes 2097168 | tf_op jit(solution)/shard_map/reduce_scatter | solution.py:38
  301.8 4.3 select_bitcast_fusion
  306.2 0.5 reshape.62
  306.7 1.1 gather_fusion
  307.8 0.7 select_convert_fusion
  308.5 0.0 all-to-all-done
  308.5 3.3 all-to-all-start.1
  311.8 0.0 all-gather.5.cloned.1.call-start
  311.9 3.9 all-to-all-done.1
  315.7 0.4 fusion
  316.1 0.1 div.10
  316.2 2.1 multiply_add_fusion
  318.3 0.0 all-gather.5.cloned.1.call-update
  318.3 0.0 all-gather.3.cloned.1.call-start
  318.4 0.7 all-gather.3.cloned.1.call-update
  319.1 20.2 %all-gather.5.cloned.1.call-done = f32[512,1024]{1,0:T(8,128)} async-done(((f32[128,1024]{1,0:T(8,128)}), f32[512,1024]{1,0:T(8,128)}) %all-gather.5.cloned.1.call-update) | async-done | bytes 2097168 | tf_op jit(solution)/shard_map/all_gather | solution.py:65
  339.3 80.7 %all-gather.3.cloned.1.call-done = bf16[4096,1024]{1,0:T(8,128)(2,1)} async-done(((bf16[128,1024]{1,0:T(8,128)(2,1)}), bf16[4096,1024]{1,0:T(8,128)(2,1)}) %all-gather.3.cloned.1.call-update) | async-done | bytes 8388624 | tf_op jit(solution)/shard_map/all_gather | solution.py:66
  420.0 0.0 copy-start.1
  420.0 8.5 %copy.13 = bf16[8,4,128,1024]{3,2,1,0:T(8,128)(2,1)} copy(bf16[8,4,128,1024]{3,2,0,1:T(8,128)(2,1)} %bitcast.28) | data formatting | bytes 16777216 | tf_op jit(solution)/shard_map/transpose | solution.py:68
  428.5 0.0 copy-done.1
  428.5 1.3 copy.15
Async XLA Ops:
  7.2 1.2 copy-start
  7.2 294.7 %reduce-scatter.2.cloned.1.call-start = ((), (), s32[]{:S(2)}) async-start(), calls=%async_computation.3 | async-start | bytes 18874368 | tf_op jit(solution)/shard_map/reduce_scatter | solution.py:38
  18.8 289.8 %all-to-all-start = ((s32[4,1,32]{2,1,0:T(1,128)}), s32[4,1,32]{2,1,0:T(1,128)S(1)}, u32[]{:S(2)}, u32[]{:S(2)}) async-start(s32[4,1,32]{2,1,0:T(1,128)} %bitcast.1), calls=%async_computation | async-start | bytes 4096 | tf_op jit(solution)/shard_map/all_to_all | solution.py:57
  308.5 7.2 %all-to-all-start.1 = ((bf16[4,32,128]{2,1,0:T(8,128)(2,1)}), bf16[4,32,128]{2,1,0:T(8,128)(2,1)S(1)}, u32[]{:S(2)}, u32[]{:S(2)}) async-start(bf16[4,32,128]{2,1,0:T(8,128)(2,1)} %select_convert_fusion), calls=%async_computation.2 | async-start | bytes 65536 | tf_op jit(solution)/shard_map/all_to_all | solution.py:56
  311.8 27.5 %all-gather.5.cloned.1.call-start = ((), (), s32[]{:S(2)}) async-start(), calls=%async_computation.5 | async-start | bytes 2621440 | tf_op jit(solution)/shard_map/all_gather | solution.py:65
  318.3 101.6 %all-gather.3.cloned.1.call-start = ((), (), s32[]{:S(2)}) async-start(), calls=%async_computation.4 | async-start | bytes 8650752 | tf_op jit(solution)/shard_map/all_gather | solution.py:66
  420.0 8.5 %copy-start.1 = (f32[512,1024]{1,0:T(8,128)S(1)}, f32[512,1024]{1,0:T(8,128)}, u32[]{:S(2)}) copy-start(f32[512,1024]{1,0:T(8,128)} %all-gather.5.cloned.1.call-done) | copy-start | bytes 6291460
Sparse Core Ops, SparseCore 0:
  18.9 282.9 reduce-scatter.1
  318.5 20.7 all-gather.4
  342.8 77.0 all-gather.2
where the time goes:
time: 437 us; the launch traced here: 436 us
  waiting for transfers between devices  381 us (87%)
  local copies, waits for them, and re-layouts  14.2 us (3%)
  between operations  13.8 us (3%)
  matrix products  10.7 us (2%)
  other arithmetic  9.44 us (2%)
  starting transfers between devices  7.65 us (2%)
    reduce_scatter x1, waiting for transfers between devices, local(): lax.psum_scatter(lax.dot_general(inputs, grad_out, (((0,), (0,)), ((), ()...  275 us
    all_gather x1, waiting for transfers between devices, local(): blocks = lax.all_gather(new_rows, ('between', 'inside'), axis=0, tiled=True)  80.7 us
    all_gather x1, waiting for transfers between devices, local(): moment = lax.all_gather(new_moment, 'between', axis=0, tiled=True)  20.2 us
    dot_general x1, matrix products, local(): lax.dot_general(inputs, grad_out, (((0,), (0,)), ((), ())), preferred_ele...  10.4 us
  transfers between devices with their start and end apart: 5, of which 4 were waited for; matrix products, arithmetic and copies ran while one was open for 2% of the time, Pallas kernels for 0%

commit v1 on v0

v1 whole, which is shorter than its diff:
```python
import math

import jax
import jax.numpy as jnp
from jax import lax
from jax.experimental import pallas as pl
from jax.experimental.pallas import tpu as pltpu
from jax.sharding import PartitionSpec as P


TILE = 128


feedback_decay = 0.95
outer_rate = 0.7
outer_momentum = 0.9


def swap(values, axis, bit):
    size = lax.axis_size(axis)
    return lax.ppermute(values, axis, [(i, i ^ (1 << bit)) for i in range(size)])


def spread(values):
    size = lax.axis_size("inside")
    every = jnp.broadcast_to(values[None], (size, *values.shape))
    return lax.all_to_all(every, "inside", split_axis=0, concat_axis=0, tiled=True)


def swap_sets(sets, bit):
    out = []
    for one in sets:
        out.append([])
        for values in one:
            out[-1].append(swap(values, "between", bit))
    return out


def dot_t(left, right):
    return lax.dot_general(left, right, (((0,), (0,)), ((), ())), preferred_element_type=jnp.float32)


def take_halves(place, x, rows_dev, chunks, first, count):
    tokens, feat = x.shape
    halves = feat // rows_dev // 2
    rows = rows_dev // chunks

    def column(k):
        return lambda h, p: (0, (2 * h + 1 - p[0]) * chunks + k)

    def body(place_ref, *refs):
        for k in range(count):
            refs[count + k][...] = refs[k][...]

    return pl.pallas_call(
        body,
        grid_spec=pltpu.PrefetchScalarGridSpec(
            num_scalar_prefetch=1,
            grid=(halves,),
            in_specs=[pl.BlockSpec((tokens, rows), column(first + k)) for k in range(count)],
            out_specs=[pl.BlockSpec((tokens, rows), lambda h, p: (0, h)) for _ in range(count)],
        ),
        out_shape=[jax.ShapeDtypeStruct((tokens, halves * rows), x.dtype) for _ in range(count)],
        name="take_halves",
    )(place, *([x] * count))


def pair_dot(place, x_own, x_recv, dy_own, dy_recv, chunk, chunks, halves):
    tokens, width = dy_own.shape
    rows = x_recv.shape[1] // halves
    quarter = halves // 2
    steps = 2
    columns = width // steps

    def own_spec(i, mine):
        def at(c, p):
            half = 2 * i + (p[1] if mine else 1 - p[1])
            return (0, (2 * half + p[0]) * chunks + chunk)

        return pl.BlockSpec((tokens, rows), at)

    def body(p, *refs):
        owns, (xr, do, dr, send, keep) = refs[: 2 * quarter], refs[2 * quarter :]
        recvs = []
        for mine in (False, True):
            for i in range(quarter):
                half = 2 * i + (p[1] if mine else 1 - p[1])
                recvs.append(xr[:, pl.ds(pl.multiple_of(half * rows, rows), rows)])
        own = jnp.concatenate([r[...] for r in owns], axis=1)
        recv = jnp.concatenate(recvs, axis=1)
        total = dot_t(own, do[...]) + dot_t(recv, dr[...])
        total = total.reshape(2, quarter, rows, columns)
        send[...] = total[0].astype(send.dtype)
        keep[...] = total[1]

    return pl.pallas_call(
        body,
        grid_spec=pltpu.PrefetchScalarGridSpec(
            num_scalar_prefetch=1,
            grid=(steps,),
            in_specs=[
                *[own_spec(i, mine) for mine in (False, True) for i in range(quarter)],
                pl.BlockSpec((tokens, halves * rows), lambda c, p: (0, 0)),
                pl.BlockSpec((tokens, columns), lambda c, p: (0, c)),
                pl.BlockSpec((tokens, columns), lambda c, p: (0, c)),
            ],
            out_specs=[pl.BlockSpec((quarter, rows, columns), lambda c, p: (0, 0, c))] * 2,
        ),
        out_shape=[
            jax.ShapeDtypeStruct((quarter, rows, width), jnp.bfloat16),
            jax.ShapeDtypeStruct((quarter, rows, width), jnp.float32),
        ],
        name="pair_dot",
    )(place, *([x_own] * (2 * quarter)), x_recv, dy_own, dy_recv)


def slot_terms(place, x, dy, index, rows_dev, own_rows):
    tokens, width = dy.shape
    tiles_row = width // TILE
    group, _, slots = index.shape
    cap = slots * own_rows // rows_dev

    def body(p, ix, xb, dyb, out, flipped):
        @pl.when(pl.program_id(0) == 0)
        def _():
            flipped[...] = dyb[...].T

        picked = []
        for side in range(2):
            at = jnp.maximum(ix[side], 0)
            owner = lax.broadcasted_iota(jnp.int32, (1, slots), 1) // cap
            row = owner * own_rows + at // tiles_row
            onehot = jnp.where(lax.broadcasted_iota(jnp.int32, (rows_dev, slots), 0) == row, 1.0, 0.0).astype(jnp.bfloat16)
            picked.append(jnp.dot(xb[:, side * rows_dev : (side + 1) * rows_dev], onehot, preferred_element_type=jnp.float32).astype(jnp.bfloat16))
        terms = jnp.dot(flipped[...], jnp.concatenate(picked, axis=1), preferred_element_type=jnp.float32)
        for side in range(2):
            column = jnp.maximum(ix[side], 0) % tiles_row
            total = jnp.zeros((TILE, slots), jnp.float32)
            for c in range(tiles_row):
                total = jnp.where(column == c, terms[c * TILE : (c + 1) * TILE, side * slots : (side + 1) * slots], total)
            out[side] = total.T.astype(jnp.bfloat16)

    return pl.pallas_call(
        body,
        grid_spec=pltpu.PrefetchScalarGridSpec(
            num_scalar_prefetch=1,
            grid=(group // 2,),
            in_specs=[
                pl.BlockSpec((2, 1, slots), lambda i, p: (i, 0, 0)),
                pl.BlockSpec((tokens, 2 * rows_dev), lambda i, p: (0, i)),
                pl.BlockSpec((tokens, width), lambda i, p: (0, 0)),
            ],
            out_specs=pl.BlockSpec((2, slots, TILE), lambda i, p: (i, 0, 0)),
            scratch_shapes=[pltpu.VMEM((width, tokens), jnp.bfloat16)],
        ),
        out_shape=jax.ShapeDtypeStruct((group, slots, TILE), jnp.bfloat16),
        name="slot_terms",
    )(place, index, x, dy)


def block_delta(ix, values, own_rows, tiles_row):
    slots = ix.shape[1]
    q = lax.broadcasted_iota(jnp.int32, (own_rows, slots), 0) * tiles_row
    onehot = [jnp.where(q == ix - c, 1.0, 0.0).astype(jnp.bfloat16) for c in range(tiles_row)]
    return jnp.dot(jnp.concatenate(onehot, axis=0), values, preferred_element_type=jnp.float32)


def momentum_step(place, momentum, index, values):
    rows_dev, width = momentum.shape
    islands, _, owners, cap, _ = values.shape
    own_rows = rows_dev // owners
    tiles_row = width // TILE
    slots = islands * cap

    def body(p, ix, v, mom, out):
        parts = block_delta(ix[0, 0], v[...].reshape(slots, TILE), own_rows, tiles_row)
        for c in range(tiles_row):
            at = slice(c * TILE, (c + 1) * TILE)
            part = parts[c * own_rows : (c + 1) * own_rows]
            out[:, at] = outer_momentum * mom[:, at] + part * (1.0 / islands)

    return pl.pallas_call(
        body,
        grid_spec=pltpu.PrefetchScalarGridSpec(
            num_scalar_prefetch=1,
            grid=(owners,),
            in_specs=[
                pl.BlockSpec((1, 1, 1, slots), lambda o, p: (p[2], o, 0, 0)),
                pl.BlockSpec((islands, 1, 1, cap, TILE), lambda o, p: (0, p[2], o, 0, 0)),
                pl.BlockSpec((own_rows, width), lambda o, p: (o, 0)),
            ],
            out_specs=pl.BlockSpec((own_rows, width), lambda o, p: (o, 0)),
        ),
        out_shape=jax.ShapeDtypeStruct(momentum.shape, jnp.float32),
        name="momentum_step",
    )(place, index, values, momentum)


def weight_step(sets, groups, where, index, values, shape, before=None):
    count, subs = len(sets), len(sets[0])
    per = sets[0][0].shape[0]
    pieces = subs * per
    halves, _, islands, own_rows, width = shape
    cap = values.shape[3]
    tiles_row = width // TILE
    slots = islands * cap
    rate = outer_rate * (1.0 + outer_momentum) / islands
    flat = [a for one in sets for a in one]

    def body(w, ix, v, *refs):
        arrays, (out, held, sems) = refs[: len(flat)], refs[-3:]
        step = pl.program_id(0)

        def copy(n):
            to = held.at[n // subs, pl.ds(n % subs * per, per)]
            return pltpu.make_async_copy(arrays[n], to, sems.at[n])

        @pl.when(step == 0)
        def _():
            for n in range(len(flat)):
                copy(n).start()

        for s in range(count):

            @pl.when(step == s)
            def _(s=s):
                for u in range(subs):
                    copy(s * subs + u).wait()

        owner = w[2 + step]
        for i in range(pieces):
            device = w[1] ^ groups[i]
            parts = block_delta(ix[device, owner], v[:, device, owner].reshape(slots, TILE), own_rows, tiles_row)
            to = device >> 1
            for c in range(tiles_row):
                at = slice(c * TILE, (c + 1) * TILE)
                part = parts[c * own_rows : (c + 1) * own_rows]
                out[to, 0, 0, :, at] = (held[step, i, :, at].astype(jnp.float32) - rate * part).astype(jnp.bfloat16)

    extra = [] if before is None else [before]
    return pl.pallas_call(
        body,
        grid_spec=pltpu.PrefetchScalarGridSpec(
            num_scalar_prefetch=1,
            grid=(count,),
            in_specs=[
                pl.BlockSpec(index.shape, lambda g, w: (0, 0, 0, 0)),
                pl.BlockSpec(values.shape, lambda g, w: (0, 0, 0, 0, 0)),
                *[pl.BlockSpec(memory_space=pl.ANY) for _ in flat + extra],
            ],
            out_specs=pl.BlockSpec((halves, 1, 1, own_rows, width), lambda g, w: (0, w[0], w[2 + g], 0, 0)),
            scratch_shapes=[
                pltpu.VMEM((count, pieces, own_rows, width), jnp.bfloat16),
                pltpu.SemaphoreType.DMA((len(flat),)),
            ],
        ),
        out_shape=jax.ShapeDtypeStruct(shape, jnp.bfloat16),
        input_output_aliases={} if before is None else {3 + len(flat): 0},
        name="weight_step",
    )(where, index, values, *flat, *extra)


def local(inputs, grad_out, error, momentum, weight, tile_index):
    group = lax.axis_size("inside")
    islands = lax.axis_size("between")
    tokens, feat = inputs.shape
    width = grad_out.shape[1]
    rows_dev = feat // group
    own_rows = rows_dev // islands
    tiles_row = width // TILE
    own_tiles = own_rows * tiles_row
    cap = tile_index.shape[3]
    inside_bits = group.bit_length() - 1
    outer_bits = [*range(1, islands.bit_length() - 1), 0]
    chunks = max(1, min(4, rows_dev // TILE))
    rows = rows_dev // chunks
    halves = group // 2
    j = lax.axis_index("inside")
    b = lax.axis_index("between")
    place = jnp.stack([j & 1, (j >> 1) & 1, j])
    index = tile_index[0, 0]

    numbers = spread(index)
    island_numbers = numbers.reshape(group, 1, islands * cap)

    dy_recv = swap(grad_out, "inside", 0)
    x_send = take_halves(place, inputs, rows_dev, chunks, 0, 1)
    if chunks > 1:
        x_send += take_halves(place, inputs, rows_dev, chunks, 1, chunks - 1)

    terms = slot_terms(place, inputs, grad_out, island_numbers, rows_dev, own_rows)
    index, terms, numbers = lax.optimization_barrier((index, terms, numbers))
    terms = lax.all_to_all(terms, "inside", split_axis=0, concat_axis=0, tiled=True)

    numbers = numbers[None]
    for bit in outer_bits:
        numbers = jnp.concatenate([numbers, swap(numbers, "between", bit)], axis=0)
    by_device = numbers.transpose(1, 2, 0, 3).reshape(group, islands, 1, islands * cap)

    start = b * own_rows
    base = (
        lax.dynamic_slice_in_dim(weight, start, own_rows, 0).astype(jnp.float32)
        - outer_rate * outer_momentum * outer_momentum * lax.dynamic_slice_in_dim(momentum, start, own_rows, 0)
    ).astype(jnp.bfloat16)[None]
    base_parts = []
    base_group = [0]
    for bit in reversed(range(1, inside_bits)):
        last = swap(base, "inside", bit)
        base_parts = [base, last]
        base = jnp.concatenate(base_parts, axis=0)
        base_group += [g ^ (1 << bit) for g in base_group]

    x_recv = []
    for k in range(chunks):
        x_recv.append(swap(x_send[k], "inside", 0))

    scale = 1.0 / math.sqrt(tokens * group)
    tiles = error[0].reshape(islands, own_tiles, TILE)
    picked = jnp.take_along_axis(tiles, jnp.maximum(index, 0)[:, :, None], axis=1)
    sums = jnp.sum(terms.astype(jnp.float32), axis=0).reshape(islands, cap, TILE)
    sent = jnp.where(index[:, :, None] >= 0, feedback_decay * picked + scale * sums, 0.0).astype(jnp.bfloat16)
    values = spread(sent)[None]
    for bit in outer_bits:
        values = jnp.concatenate([values, swap(values, "between", bit)], axis=0)

    across = []
    for part in base_parts:
        across.append(swap(part, "inside", 0))
    near_sets, far_sets = [[base]], [across]
    owners = [0]
    for bit in outer_bits:
        near_sets += swap_sets(near_sets, bit)
        far_sets += swap_sets(far_sets, bit)
        owners += [o ^ (1 << bit) for o in owners]
    set_owner = [b ^ o for o in owners]
    new_weight = None
    for parity, sets in enumerate((near_sets, far_sets)):
        gone = [g ^ parity for g in base_group]
        where = jnp.stack([(j & 1) ^ parity, j, *set_owner])
        new_weight = weight_step(
            sets, gone, where, by_device, values,
            (halves, 2, islands, own_rows, width), new_weight,
        )
    new_weight = new_weight.reshape(feat, width)
    new_momentum = momentum_step(place, momentum, by_device, values)

    hit = jnp.any(index[:, None, None, :] == jnp.arange(own_tiles, dtype=jnp.int32).reshape(1, own_rows, tiles_row, 1), axis=3)
    free = jnp.where(hit.reshape(rows_dev, tiles_row, 1), 0.0, 1.0)
    free = jnp.broadcast_to(free, (rows_dev, tiles_row, TILE)).reshape(rows_dev, width)
    parts = []
    for k in range(chunks):
        send, keep = pair_dot(place, inputs, x_recv[k], grad_out, dy_recv, k, chunks, halves)
        current = keep + swap(send, "inside", 1).astype(jnp.float32)
        for bit in range(2, inside_bits):
            mine = (j >> bit) & 1
            current = current.reshape(current.shape[0] // 2, 2, rows, width)
            send = lax.dynamic_index_in_dim(current, 1 - mine, 1, keepdims=False).astype(jnp.bfloat16)
            keep = lax.dynamic_index_in_dim(current, mine, 1, keepdims=False)
            current = keep + swap(send, "inside", bit).astype(jnp.float32)
        parts.append(current[0])
    grad = jnp.concatenate(parts, axis=0)
    new_error = (free * (feedback_decay * error[0] + scale * grad))[None]
    return (new_weight, new_momentum, new_error)


def solution(mesh):
    in_specs = (
        P(("between", "inside"), None),
        P(("between", "inside"), None),
        P("between", "inside", None),
        P("inside", None),
        P("inside", None),
        P("between", "inside", None, None),
    )
    out_specs = (P(), P("inside", None), P("between", "inside", None))
    return jax.shard_map(local, mesh=mesh, in_specs=in_specs, out_specs=out_specs, check_vma=False)
```

time: 437 us -> 202 us (0.46)
  waiting for transfers between devices: 381 us -> 69.5 us
  Pallas kernels: 0 us -> 53.4 us
  starting transfers between devices: 7.65 us -> 43.4 us
  between operations: 13.8 us -> 1.22 us
  matrix products: 10.7 us -> 0 us
  other arithmetic: 9.44 us -> 17.2 us
    reduce_scatter x1 -> x0, waiting for transfers between devices: 275 us -> none  [local(): lax.psum_scatter(lax.dot_general(inputs, grad_out, (((0,), (0,)), ((), ()...]
    all_gather x2 -> x0, waiting for transfers between devices: 101 us -> none  [the longest x1 80.7 us: local(): blocks = lax.all_gather(new_rows, ('between', 'inside'), axis=0, tiled=True)]
    ppermute x0 -> x30, waiting for transfers between devices: none -> 55.5 us  [swap(): return lax.ppermute(values, axis, [(i, i ^ 1 << bit) for i in range(size)])]
    pallas_call x0 -> x10, Pallas kernels: none -> 53.4 us  [the longest x4 18.8 us: pair_dot(): pl.pallas_call(body, grid_spec=pltpu.PrefetchScalarGridSpec(num_scalar_pr...]
    ppermute x0 -> x30, starting transfers between devices: none -> 29.1 us  [swap(): return lax.ppermute(values, axis, [(i, i ^ 1 << bit) for i in range(size)])]
    dot_general x2 -> x0, matrix products: 10.7 us -> none  [the longest x1 10.4 us: local(): lax.dot_general(inputs, grad_out, (((0,), (0,)), ((), ())), preferred_ele...]
    all_to_all x2 -> x3, waiting for transfers between devices: 3.86 us -> 14 us  [the longest x2 14 us: spread(): lax.all_to_all(every, 'inside', split_axis=0, concat_axis=0, tiled=True)]
    transpose x1 -> x0, local copies, waits for them, and re-layouts: 8.52 us -> none  [local(): blocks.reshape(islands, group, own_rows, width).transpose(1, 0, 2, 3)]
  transfers between devices with their start and end apart: 5 -> 33, of which waited for: 4 -> 11; matrix products, arithmetic and copies ran while one was open for 2% -> 15% of each run, Pallas kernels for 0% -> 23%
where the time goes in v1:
time: 202 us; the launch traced here: 201 us
  waiting for transfers between devices  69.5 us (34%)
  Pallas kernels  53.4 us (26%)
  starting transfers between devices  43.4 us (21%)
  other arithmetic  17.2 us (9%)
  local copies, waits for them, and re-layouts  16.4 us (8%)
    ppermute x30, waiting for transfers between devices, swap(): return lax.ppermute(values, axis, [(i, i ^ 1 << bit) for i in range(size)])  55.5 us
    ppermute x30, starting transfers between devices, swap(): return lax.ppermute(values, axis, [(i, i ^ 1 << bit) for i in range(size)])  29.1 us
    pallas_call x4, Pallas kernels, pair_dot(): pl.pallas_call(body, grid_spec=pltpu.PrefetchScalarGridSpec(num_scalar_pr...  18.8 us
    pallas_call x2, Pallas kernels, weight_step(): pl.pallas_call(body, grid_spec=pltpu.PrefetchScalarGridSpec(num_scalar_pr...  14.1 us
    all_to_all x2, waiting for transfers between devices, spread(): lax.all_to_all(every, 'inside', split_axis=0, concat_axis=0, tiled=True)  14 us
    all_to_all x2, starting transfers between devices, spread(): lax.all_to_all(every, 'inside', split_axis=0, concat_axis=0, tiled=True)  10.9 us
    pallas_call x2, Pallas kernels, take_halves(): pl.pallas_call(body, grid_spec=pltpu.PrefetchScalarGridSpec(num_scalar_pr...  8.31 us
    pallas_call x1, Pallas kernels, slot_terms(): pl.pallas_call(body, grid_spec=pltpu.PrefetchScalarGridSpec(num_scalar_pr...  7.31 us
  transfers between devices with their start and end apart: 33, of which 11 were waited for; matrix products, arithmetic and copies ran while one was open for 15% of the time, Pallas kernels for 23%

profile of v1, /device:TPU:0, one launch (start us, length us, event | category | flops | bytes accessed | tf_op | source)
XLA Modules:
  0.0 201.0 jit_solution(7703635526843397679)
XLA Ops:
  2.0 7.3 %all-to-all-start = ((s32[8,1,128]{2,1,0:T(1,128)}), s32[8,1,128]{2,1,0:T(1,128)S(1)}, u32[]{:S(2)}, u32[]{:S(2)}) async-start(s32[8,1,128]{2,1,0:T(1,128)} %reshape.170), calls=%async_computation | async-start | bytes 8192 | tf_op jit(solution)/shard_map/all_to_all | solution.py:27
  9.3 2.0 %collective-permute-start.18 = (bf16[512,1024]{1,0:T(8,128)(2,1)}, bf16[512,1024]{1,0:T(8,128)(2,1)S(1)}, u32[]{:S(2)}, u32[]{:S(2)}) collective-permute-start(bf16[512,1024]{1,0:T(8,128)(2,1)} %refs_5_.7), channel_id=1, source_target_pairs={{0,1},{1,0},{2,3},{3,2},{4,5},{5,4},{6,7},{7,6},{8,9},{9,8},{10,11... | collective-permute-start | bytes 3145736 | tf_op jit(solution)/shard_map/ppermute | solution.py:21
  11.9 3.8 %all-to-all-done = s32[8,1,128]{2,1,0:T(1,128)S(1)} async-done(((s32[8,1,128]{2,1,0:T(1,128)}), s32[8,1,128]{2,1,0:T(1,128)S(1)}, u32[]{:S(2)}, u32[]{:S(2)}) %all-to-all-start) | async-done | bytes 4128 | tf_op jit(solution)/shard_map/all_to_all | solution.py:27
  17.6 7.3 %slot_terms.1 = bf16[8,128,128]{2,1,0:T(8,128)(2,1)} custom-call(s32[3]{0:T(128)} %pad_add_fusion.1.p.place_ref, s32[8,1,128]{2,1,0:T(1,128)} %reshape.149.ix, bf16[512,4096]{1,0:T(8,128)(2,1)} %refs_3_.7, bf16[512,1024]{1,0:T(8,128)(2,1)} %refs_5_.7), custom_call_target="tpu_custom_call" | custom-call | tf_op jit(solution)/shard_map/slot_terms/pallas_call | solution.py:143
  25.0 3.4 %all-to-all-start.1 = ((bf16[8,128,128]{2,1,0:T(8,128)(2,1)}), bf16[8,128,128]{2,1,0:T(8,128)(2,1)S(1)}, u32[]{:S(2)}, u32[]{:S(2)}) async-start(bf16[8,128,128]{2,1,0:T(8,128)(2,1)} %slot_terms.1), calls=%async_computation.1 | async-start | bytes 524288 | tf_op jit(solution)/shard_map/all_to_all | solution.py:293
  28.4 1.9 fusion.2
  30.3 2.8 %collective-permute-start.4 = (bf16[1,128,1024]{2,1,0:T(8,128)(2,1)}, bf16[1,128,1024]{2,1,0:T(8,128)(2,1)}, u32[]{:S(2)}, u32[]{:S(2)}) collective-permute-start(bf16[1,128,1024]{2,1,0:T(8,128)(2,1)} %fusion.2), channel_id=1, source_target_pairs={{0,4},{1,5},{2,6},{3,7},{4,0},{5,1},{6,2},{7,3},{8,12},{9,13},{10,... | collective-permute-start | bytes 786440 | tf_op jit(solution)/shard_map/ppermute | solution.py:21
  33.1 4.3 %take_halves.3 = (bf16[512,512]{1,0:T(8,128)(2,1)}, bf16[512,512]{1,0:T(8,128)(2,1)}, bf16[512,512]{1,0:T(8,128)(2,1)}) custom-call(s32[3]{0:T(128)} %pad_add_fusion.1.p.place_ref, bf16[512,4096]{1,0:T(8,128)(2,1)} %refs_3_.7, bf16[512,4096]{1,0:T(8,128)(2,1)} %refs_3_.7, bf16[512,4096]{1,0:T(8,128)(2,1)} %refs_3_.7), custom_call_target="tpu_custom_call" | custom-call | tf_op jit(solution)/shard_map/take_halves/pallas_call | solution.py:55
  37.4 1.5 collective-permute-start.27
  39.4 1.5 collective-permute-start.21
  40.9 4.0 %take_halves.2 = bf16[512,512]{1,0:T(8,128)(2,1)} custom-call(s32[3]{0:T(128)} %pad_add_fusion.1.p.place_ref, bf16[512,4096]{1,0:T(8,128)(2,1)} %refs_3_.7), custom_call_target="tpu_custom_call" | custom-call | tf_op jit(solution)/shard_map/take_halves/pallas_call | solution.py:55
  46.1 1.5 reshape_squeeze.3
  47.6 2.6 %gather_fusion = f32[128,128]{1,0:T(8,128)S(1)} fusion(f32[4,1024,128]{2,1,0:T(8,128)} %reshape_squeeze.3, s32[128]{0:T(128)S(1)} %reshape.156), kind=kCustom, calls=%fused_computation | custom fusion | bytes 132096 | tf_op jit(solution)/shard_map/jit(take_along_axis)/gather | solution.py:319
  51.2 3.6 %all-to-all-start.2 = ((bf16[8,4,32,128]{3,2,1,0:T(8,128)(2,1)}), bf16[8,4,32,128]{3,2,1,0:T(8,128)(2,1)S(1)}, u32[]{:S(2)}, u32[]{:S(2)}) async-start(bf16[8,4,32,128]{3,2,1,0:T(8,128)(2,1)} %broadcast_in_dim.63), calls=%async_computation.2 | async-start | bytes 524288 | tf_op jit(solution)/shard_map/all_to_all | solution.py:27
  54.8 1.4 collective-permute-start
  56.1 1.9 pad_maximum_fusion.3
  58.6 1.7 collective-permute-start.6
  60.4 1.5 collective-permute-start.17
  62.9 4.6 %pair_dot.7 = (bf16[2,128,1024]{2,1,0:T(8,128)(2,1)}, f32[2,128,1024]{2,1,0:T(8,128)}) custom-call(s32[3]{0:T(128)} %pad_add_fusion.1.p.place_ref, bf16[512,4096]{1,0:T(8,128)(2,1)} %refs_3_.7, bf16[512,4096]{1,0:T(8,128)(2,1)} %refs_3_.7, bf16[512,4096]{1,0:T(8,128)(2,1)} %refs_3_.7, bf16[512,4096]{1,0:T(8,128)(2,1)} %refs_3_.7, ...), custom_call_target="tpu_custom_call" | custom-call | tf_op jit(solution)/shard_map/pair_dot/pallas_call | solution.py:96
  67.5 10.2 %all-to-all-done.2 = bf16[8,4,32,128]{3,2,1,0:T(8,128)(2,1)S(1)} async-done(((bf16[8,4,32,128]{3,2,1,0:T(8,128)(2,1)}), bf16[8,4,32,128]{3,2,1,0:T(8,128)(2,1)S(1)}, u32[]{:S(2)}, u32[]{:S(2)}) %all-to-all-start.2) | async-done | bytes 262176 | tf_op jit(solution)/shard_map/all_to_all | solution.py:27
  77.7 1.5 collective-permute-start.2
  79.2 1.8 collective-permute-start.28
  81.8 1.5 reshape.155
  84.0 4.7 %pair_dot.6 = (bf16[2,128,1024]{2,1,0:T(8,128)(2,1)}, f32[2,128,1024]{2,1,0:T(8,128)}) custom-call(s32[3]{0:T(128)} %pad_add_fusion.1.p.place_ref, bf16[512,4096]{1,0:T(8,128)(2,1)} %refs_3_.7, bf16[512,4096]{1,0:T(8,128)(2,1)} %refs_3_.7, bf16[512,4096]{1,0:T(8,128)(2,1)} %refs_3_.7, bf16[512,4096]{1,0:T(8,128)(2,1)} %refs_3_.7, ...), custom_call_target="tpu_custom_call" | custom-call | tf_op jit(solution)/shard_map/pair_dot/pallas_call | solution.py:96
  89.0 1.3 pad_maximum_fusion.1.refs_0_
  90.3 1.9 collective-permute-start.5
  92.2 4.7 %pair_dot.5 = (bf16[2,128,1024]{2,1,0:T(8,128)(2,1)}, f32[2,128,1024]{2,1,0:T(8,128)}) custom-call(s32[3]{0:T(128)} %pad_add_fusion.1.p.place_ref, bf16[512,4096]{1,0:T(8,128)(2,1)} %refs_3_.7, bf16[512,4096]{1,0:T(8,128)(2,1)} %refs_3_.7, bf16[512,4096]{1,0:T(8,128)(2,1)} %refs_3_.7, bf16[512,4096]{1,0:T(8,128)(2,1)} %refs_3_.7, ...), custom_call_target="tpu_custom_call" | custom-call | tf_op jit(solution)/shard_map/pair_dot/pallas_call | solution.py:96
  97.6 4.7 %pair_dot.4 = (bf16[2,128,1024]{2,1,0:T(8,128)(2,1)}, f32[2,128,1024]{2,1,0:T(8,128)}) custom-call(s32[3]{0:T(128)} %pad_add_fusion.1.p.place_ref, bf16[512,4096]{1,0:T(8,128)(2,1)} %refs_3_.7, bf16[512,4096]{1,0:T(8,128)(2,1)} %refs_3_.7, bf16[512,4096]{1,0:T(8,128)(2,1)} %refs_3_.7, bf16[512,4096]{1,0:T(8,128)(2,1)} %refs_3_.7, ...), custom_call_target="tpu_custom_call" | custom-call | tf_op jit(solution)/shard_map/pair_dot/pallas_call | solution.py:96
  102.4 1.1 pad_maximum_fusion.2
  103.5 1.2 collective-permute-start.22
  104.6 1.3 convert_add_fusion
  107.1 10.6 %collective-permute-done.22 = bf16[2,128,1024]{2,1,0:T(8,128)(2,1)S(1)} collective-permute-done((bf16[2,128,1024]{2,1,0:T(8,128)(2,1)S(1)}, bf16[2,128,1024]{2,1,0:T(8,128)(2,1)S(1)}, u32[]{:S(2)}, u32[]{:S(2)}) %collective-permute-start.22) | collective-permute-done | bytes 524320 | tf_op jit(solution)/shard_map/ppermute | solution.py:21
  117.8 1.1 collective-permute-start.19
  120.7 10.5 %collective-permute-done.19 = bf16[2,128,1024]{2,1,0:T(8,128)(2,1)S(1)} collective-permute-done((bf16[2,128,1024]{2,1,0:T(8,128)(2,1)S(1)}, bf16[2,128,1024]{2,1,0:T(8,128)(2,1)S(1)}, u32[]{:S(2)}, u32[]{:S(2)}) %collective-permute-start.19) | collective-permute-done | bytes 524320 | tf_op jit(solution)/shard_map/ppermute | solution.py:21
  131.6 2.7 %collective-permute-start.26 = (bf16[1,128,1024]{2,1,0:T(8,128)(2,1)}, bf16[1,128,1024]{2,1,0:T(8,128)(2,1)}, u32[]{:S(2)}, u32[]{:S(2)}) collective-permute-start(bf16[1,128,1024]{2,1,0:T(8,128)(2,1)} %dynamic-slice_convert_fusion.1), channel_id=1, source_target_pairs={{0,4},{1,5},{2,6},{3,7},{4,0},{5,1},{6,2},{7,3},{8,12},{9,13},{10,... | collective-permute-start | bytes 786440 | tf_op jit(solution)/shard_map/ppermute | solution.py:21
  136.1 2.0 %pad_maximum_fusion.v = bf16[4,8,4,32,128]{4,3,2,1,0:T(8,128)(2,1)} fusion(bf16[2,8,4,32,128]{4,3,2,1,0:T(8,128)(2,1)S(1)} %collective-permute-done.3, bf16[1,8,4,32,128]{4,3,2,1,0:T(8,128)(2,1)} %collective-permute-done.2, bf16[1,8,4,32,128]{4,3,2,1,0:T(8,128)(2,1)S(1)} %bitcast.27), kind=kLoop, calls=%fused_computation.4 | loop fusion | flops 1048576 | bytes 2097152 | tf_op jit(solution)/shard_map/concatenate | solution.py:324
  138.1 4.9 %momentum_step.1 = f32[512,1024]{1,0:T(8,128)} custom-call(s32[3]{0:T(128)} %pad_add_fusion.1.p.place_ref, s32[8,4,1,128]{3,2,1,0:T(1,128)} %reshape.150.ix, bf16[4,8,4,32,128]{4,3,2,1,0:T(8,128)(2,1)} %pad_maximum_fusion.v, f32[512,1024]{1,0:T(8,128)} %mom.1), custom_call_target="tpu_custom_call" | custom-call | tf_op jit(solution)/shard_map/momentum_step/pallas_call | solution.py:182
  143.0 15.7 %collective-permute-done.29 = bf16[1,128,1024]{2,1,0:T(8,128)(2,1)} collective-permute-done((bf16[1,128,1024]{2,1,0:T(8,128)(2,1)}, bf16[1,128,1024]{2,1,0:T(8,128)(2,1)}, u32[]{:S(2)}, u32[]{:S(2)}) %collective-permute-start.29) | collective-permute-done | bytes 262176 | tf_op jit(solution)/shard_map/ppermute | solution.py:21
  158.7 1.5 collective-permute-start.8
  160.2 4.1 %collective-permute-done.26 = bf16[1,128,1024]{2,1,0:T(8,128)(2,1)} collective-permute-done((bf16[1,128,1024]{2,1,0:T(8,128)(2,1)}, bf16[1,128,1024]{2,1,0:T(8,128)(2,1)}, u32[]{:S(2)}, u32[]{:S(2)}) %collective-permute-start.26) | collective-permute-done | bytes 262176 | tf_op jit(solution)/shard_map/ppermute | solution.py:21
  164.3 1.5 collective-permute-start.9
  165.8 1.3 convert_add_fusion.4
  167.2 2.3 %collective-permute-done.23 = bf16[1,128,1024]{2,1,0:T(8,128)(2,1)} collective-permute-done((bf16[1,128,1024]{2,1,0:T(8,128)(2,1)}, bf16[1,128,1024]{2,1,0:T(8,128)(2,1)}, u32[]{:S(2)}, u32[]{:S(2)}) %collective-permute-start.23) | collective-permute-done | bytes 262176 | tf_op jit(solution)/shard_map/ppermute | solution.py:21
  171.5 2.3 %collective-permute-done.8.refs_2_ = bf16[2,128,1024]{2,1,0:T(8,128)(2,1)} collective-permute-done((bf16[2,128,1024]{2,1,0:T(8,128)(2,1)}, bf16[2,128,1024]{2,1,0:T(8,128)(2,1)}, u32[]{:S(2)}, u32[]{:S(2)}) %collective-permute-start.8) | collective-permute-done | bytes 524320 | tf_op jit(solution)/shard_map/ppermute | solution.py:21
  173.8 9.2 %collective-permute-done.20 = bf16[1,128,1024]{2,1,0:T(8,128)(2,1)S(1)} collective-permute-done((bf16[1,128,1024]{2,1,0:T(8,128)(2,1)}, bf16[1,128,1024]{2,1,0:T(8,128)(2,1)S(1)}, u32[]{:S(2)}, u32[]{:S(2)}) %collective-permute-start.20) | collective-permute-done | bytes 262176 | tf_op jit(solution)/shard_map/ppermute | solution.py:21
  183.9 2.0 %fusion.1 = f32[1,512,1024]{2,1,0:T(8,128)} fusion(f32[1,512,1024]{2,1,0:T(8,128)S(1)} %copy-done.3, f32[1,128,1024]{2,1,0:T(8,128)S(1)} %convert_add_fusion.4, f32[1,128,1024]{2,1,0:T(8,128)S(1)} %convert_add_fusion.5, f32[1,128,1024]{2,1,0:T(8,128)S(1)} %convert_add_fusion.6, f32[1,128,1024]{2,1,0:T(8,128)S(1)} %convert_add_fusion.7, ...), kind=kLoop, calls=%fused_computation.3 | loop fusion | flops 3670016 | bytes 8388608 | tf_op jit(solution)/shard_map/mul | solution.py:362
  185.9 7.0 %weight_step.2.refs_8_ = bf16[4,2,4,128,1024]{4,3,2,1,0:T(8,128)(2,1)} custom-call(s32[6]{0:T(128)} %stack.50.w, s32[8,4,1,128]{3,2,1,0:T(1,128)} %reshape.150.ix, bf16[4,8,4,32,128]{4,3,2,1,0:T(8,128)(2,1)} %pad_maximum_fusion.v, bf16[4,128,1024]{2,1,0:T(8,128)(2,1)} %copy-done.4, bf16[4,128,1024]{2,1,0:T(8,128)(2,1)} %collective-permute-done.14.refs_1_, ...), custom_call_target="tpu_custom_call" | custom-call | tf_op jit(solution)/shard_map/weight_step/pallas_call | solution.py:241
  193.8 7.1 %weight_step.3 = bf16[4,2,4,128,1024]{4,3,2,1,0:T(8,128)(2,1)} custom-call(s32[6]{0:T(128)} %stack.46.w, s32[8,4,1,128]{3,2,1,0:T(1,128)} %reshape.150.ix, bf16[4,8,4,32,128]{4,3,2,1,0:T(8,128)(2,1)} %pad_maximum_fusion.v, bf16[2,128,1024]{2,1,0:T(8,128)(2,1)} %collective-permute-done.5.refs_0_, ...), custom_call_target="tpu_custom_call", output_to_operand_aliasing={{}: (11, {})} | custom-call | tf_op jit(solution)/shard_map/weight_step/pallas_call | solution.py:241
  (107 shorter events, 19.3 us)
Async XLA Ops:
  2.0 13.7 %all-to-all-start = ((s32[8,1,128]{2,1,0:T(1,128)}), s32[8,1,128]{2,1,0:T(1,128)S(1)}, u32[]{:S(2)}, u32[]{:S(2)}) async-start(s32[8,1,128]{2,1,0:T(1,128)} %reshape.170), calls=%async_computation | async-start | bytes 8192 | tf_op jit(solution)/shard_map/all_to_all | solution.py:27
  9.3 52.6 %collective-permute-start.18 = (bf16[512,1024]{1,0:T(8,128)(2,1)}, bf16[512,1024]{1,0:T(8,128)(2,1)S(1)}, u32[]{:S(2)}, u32[]{:S(2)}) collective-permute-start(bf16[512,1024]{1,0:T(8,128)(2,1)} %refs_5_.7), channel_id=1, source_target_pairs={{0,1},{1,0},{2,3},{3,2},{4,5},{5,4},{6,7},{7,6},{8,9},{9,8},{10,11... | collective-permute-start | bytes 3145736 | tf_op jit(solution)/shard_map/ppermute | solution.py:21
  25.0 25.3 %all-to-all-start.1 = ((bf16[8,128,128]{2,1,0:T(8,128)(2,1)}), bf16[8,128,128]{2,1,0:T(8,128)(2,1)S(1)}, u32[]{:S(2)}, u32[]{:S(2)}) async-start(bf16[8,128,128]{2,1,0:T(8,128)(2,1)} %slot_terms.1), calls=%async_computation.1 | async-start | bytes 524288 | tf_op jit(solution)/shard_map/all_to_all | solution.py:293
  30.3 24.5 %collective-permute-start.4 = (bf16[1,128,1024]{2,1,0:T(8,128)(2,1)}, bf16[1,128,1024]{2,1,0:T(8,128)(2,1)}, u32[]{:S(2)}, u32[]{:S(2)}) collective-permute-start(bf16[1,128,1024]{2,1,0:T(8,128)(2,1)} %fusion.2), channel_id=1, source_target_pairs={{0,4},{1,5},{2,6},{3,7},{4,0},{5,1},{6,2},{7,3},{8,12},{9,13},{10,... | collective-permute-start | bytes 786440 | tf_op jit(solution)/shard_map/ppermute | solution.py:21
  37.4 23.0 %collective-permute-start.27 = (bf16[512,512]{1,0:T(8,128)(2,1)}, bf16[512,512]{1,0:T(8,128)(2,1)}, u32[]{:S(2)}, u32[]{:S(2)}) collective-permute-start(bf16[512,512]{1,0:T(8,128)(2,1)} %get-tuple-element.28), channel_id=1, source_target_pairs={{0,1},{1,0},{2,3},{3,2},{4,5},{5,4},{6,7},{7,6},{8,9},{9,8},{10,11... | collective-permute-start | bytes 1572872 | tf_op jit(solution)/shard_map/ppermute | solution.py:21
  38.9 40.3 %collective-permute-start.24 = (bf16[512,512]{1,0:T(8,128)(2,1)}, bf16[512,512]{1,0:T(8,128)(2,1)}, u32[]{:S(2)}, u32[]{:S(2)}) collective-permute-start(bf16[512,512]{1,0:T(8,128)(2,1)} %get-tuple-element.25), channel_id=1, source_target_pairs={{0,1},{1,0},{2,3},{3,2},{4,5},{5,4},{6,7},{7,6},{8,9},{9,8},{10,11... | collective-permute-start | bytes 1572872 | tf_op jit(solution)/shard_map/ppermute | solution.py:21
  39.4 50.9 %collective-permute-start.21 = (bf16[512,512]{1,0:T(8,128)(2,1)}, bf16[512,512]{1,0:T(8,128)(2,1)}, u32[]{:S(2)}, u32[]{:S(2)}) collective-permute-start(bf16[512,512]{1,0:T(8,128)(2,1)} %get-tuple-element.22), channel_id=1, source_target_pairs={{0,1},{1,0},{2,3},{3,2},{4,5},{5,4},{6,7},{7,6},{8,9},{9,8},{10,11... | collective-permute-start | bytes 1572872 | tf_op jit(solution)/shard_map/ppermute | solution.py:21
  40.9 5.2 %copy-start.1 = (f32[1,512,1024]{2,1,0:T(8,128)S(1)}, f32[1,512,1024]{2,1,0:T(8,128)}, u32[]{:S(2)}) copy-start(f32[1,512,1024]{2,1,0:T(8,128)} %param.8) | copy-start | bytes 6291460
  46.1 1.5 copy-start.14
  51.2 26.5 %all-to-all-start.2 = ((bf16[8,4,32,128]{3,2,1,0:T(8,128)(2,1)}), bf16[8,4,32,128]{3,2,1,0:T(8,128)(2,1)S(1)}, u32[]{:S(2)}, u32[]{:S(2)}) async-start(bf16[8,4,32,128]{3,2,1,0:T(8,128)(2,1)} %broadcast_in_dim.63), calls=%async_computation.2 | async-start | bytes 524288 | tf_op jit(solution)/shard_map/all_to_all | solution.py:27
  54.8 3.8 %collective-permute-start = (s32[1,8,4,32]{3,0,2,1:T(1,128)S(1)}, s32[1,8,4,32]{3,0,2,1:T(1,128)S(1)}, u32[]{:S(2)}, u32[]{:S(2)}) collective-permute-start(s32[1,8,4,32]{3,0,2,1:T(1,128)S(1)} %bitcast.30), channel_id=1, source_target_pairs={{0,16},{8,24},{16,0},{24,8},{1,17},{9,25},{17,1},{25,9},{2,18},{10... | collective-permute-start | bytes 12296 | tf_op jit(solution)/shard_map/ppermute | solution.py:21
  58.6 30.1 %collective-permute-start.6 = (bf16[2,128,1024]{2,1,0:T(8,128)(2,1)}, bf16[2,128,1024]{2,1,0:T(8,128)(2,1)}, u32[]{:S(2)}, u32[]{:S(2)}) collective-permute-start(bf16[2,128,1024]{2,1,0:T(8,128)(2,1)} %pad_maximum_fusion.3), channel_id=1, source_target_pairs={{0,2},{1,3},{2,0},{3,1},{4,6},{5,7},{6,4},{7,5},{8,10},{9,11},{10,... | collective-permute-start | bytes 1572872 | tf_op jit(solution)/shard_map/ppermute | solution.py:21
  60.4 36.6 %collective-permute-start.17 = (bf16[512,512]{1,0:T(8,128)(2,1)}, bf16[512,512]{1,0:T(8,128)(2,1)}, u32[]{:S(2)}, u32[]{:S(2)}) collective-permute-start(bf16[512,512]{1,0:T(8,128)(2,1)} %take_halves.2), channel_id=1, source_target_pairs={{0,1},{1,0},{2,3},{3,2},{4,5},{5,4},{6,7},{7,6},{8,9},{9,8},{10,11... | collective-permute-start | bytes 1572872 | tf_op jit(solution)/shard_map/ppermute | solution.py:21
  61.9 5.6 %collective-permute-start.1 = (s32[2,8,4,32]{3,0,2,1:T(2,128)S(1)}, s32[2,8,4,32]{3,0,2,1:T(2,128)S(1)}, u32[]{:S(2)}, u32[]{:S(2)}) collective-permute-start(s32[2,8,4,32]{3,0,2,1:T(2,128)S(1)} %pad_add_fusion), channel_id=1, source_target_pairs={{0,8},{8,0},{16,24},{24,16},{1,9},{9,1},{17,25},{25,17},{2,10},{10... | collective-permute-start | bytes 24584 | tf_op jit(solution)/shard_map/ppermute | solution.py:21
  77.7 24.6 %collective-permute-start.2 = (bf16[1,8,4,32,128]{4,3,2,1,0:T(8,128)(2,1)S(1)}, bf16[1,8,4,32,128]{4,3,2,1,0:T(8,128)(2,1)}, u32[]{:S(2)}, u32[]{:S(2)}) collective-permute-start(bf16[1,8,4,32,128]{4,3,2,1,0:T(8,128)(2,1)S(1)} %bitcast.25), channel_id=1, source_target_pairs={{0,16},{8,24},{16,0},{24,8},{1,17},{9,25},{17,1},{25,9},{2,18},{10... | collective-permute-start | bytes 786440 | tf_op jit(solution)/shard_map/ppermute | solution.py:21
  79.2 24.2 %collective-permute-start.28 = (bf16[2,128,1024]{2,1,0:T(8,128)(2,1)}, bf16[2,128,1024]{2,1,0:T(8,128)(2,1)}, u32[]{:S(2)}, u32[]{:S(2)}) collective-permute-start(bf16[2,128,1024]{2,1,0:T(8,128)(2,1)} %get-tuple-element.30), channel_id=1, source_target_pairs={{0,2},{1,3},{2,0},{3,1},{4,6},{5,7},{6,4},{7,5},{8,10},{9,11},{10,... | collective-permute-start | bytes 1572872 | tf_op jit(solution)/shard_map/ppermute | solution.py:21
  88.7 17.3 %collective-permute-start.25 = (bf16[2,128,1024]{2,1,0:T(8,128)(2,1)}, bf16[2,128,1024]{2,1,0:T(8,128)(2,1)S(1)}, u32[]{:S(2)}, u32[]{:S(2)}) collective-permute-start(bf16[2,128,1024]{2,1,0:T(8,128)(2,1)} %get-tuple-element.27), channel_id=1, source_target_pairs={{0,2},{1,3},{2,0},{3,1},{4,6},{5,7},{6,4},{7,5},{8,10},{9,11},{10,... | collective-permute-start | bytes 1572872 | tf_op jit(solution)/shard_map/ppermute | solution.py:21
  90.3 12.0 %copy-start.4 = (bf16[4,128,1024]{2,1,0:T(8,128)(2,1)}, bf16[4,128,1024]{2,1,0:T(8,128)(2,1)S(1)}, u32[]{:S(2)}) copy-start(bf16[4,128,1024]{2,1,0:T(8,128)(2,1)S(1)} %pad_maximum_fusion.1.refs_0_) | copy-start | bytes 3145732
  90.3 41.1 %collective-permute-start.5 = (bf16[2,128,1024]{2,1,0:T(8,128)(2,1)}, bf16[2,128,1024]{2,1,0:T(8,128)(2,1)}, u32[]{:S(2)}, u32[]{:S(2)}) collective-permute-start(bf16[2,128,1024]{2,1,0:T(8,128)(2,1)} %pad_maximum_fusion.3), channel_id=1, source_target_pairs={{0,1},{1,0},{2,3},{3,2},{4,5},{5,4},{6,7},{7,6},{8,9},{9,8},{10,11... | collective-permute-start | bytes 1572872 | tf_op jit(solution)/shard_map/ppermute | solution.py:21
  97.0 6.5 %copy-start.16 = (bf16[2,128,1024]{2,1,0:T(8,128)(2,1)S(1)}, bf16[2,128,1024]{2,1,0:T(8,128)(2,1)}, u32[]{:S(2)}) copy-start(bf16[2,128,1024]{2,1,0:T(8,128)(2,1)} %get-tuple-element.24) | copy-start | bytes 1572868
  97.0 7.7 %copy-start.8 = (f32[2,128,1024]{2,1,0:T(8,128)S(1)}, f32[2,128,1024]{2,1,0:T(8,128)}, u32[]{:S(2)}) copy-start(f32[2,128,1024]{2,1,0:T(8,128)} %get-tuple-element.29) | copy-start | bytes 3145732
  97.0 72.5 %collective-permute-start.14 = (bf16[4,128,1024]{2,1,0:T(8,128)(2,1)S(1)}, bf16[4,128,1024]{2,1,0:T(8,128)(2,1)}, u32[]{:S(2)}, u32[]{:S(2)}) collective-permute-start(bf16[4,128,1024]{2,1,0:T(8,128)(2,1)S(1)} %pad_maximum_fusion.1.refs_0_), channel_id=1, source_target_pairs={{0,16},{8,24},{16,0},{24,8},{1,17},{9,25},{17,1},{25,9},{2,18},{10... | collective-permute-start | bytes 3145736 | tf_op jit(solution)/shard_map/ppermute | solution.py:21
  102.3 4.7 %copy-start.9 = (f32[2,128,1024]{2,1,0:T(8,128)S(1)}, f32[2,128,1024]{2,1,0:T(8,128)}, u32[]{:S(2)}) copy-start(f32[2,128,1024]{2,1,0:T(8,128)} %get-tuple-element.26) | copy-start | bytes 3145732
  102.3 81.3 %collective-permute-start.15 = (bf16[4,128,1024]{2,1,0:T(8,128)(2,1)S(1)}, bf16[4,128,1024]{2,1,0:T(8,128)(2,1)}, u32[]{:S(2)}, u32[]{:S(2)}) collective-permute-start(bf16[4,128,1024]{2,1,0:T(8,128)(2,1)S(1)} %pad_maximum_fusion.1.refs_0_), channel_id=1, source_target_pairs={{0,8},{8,0},{16,24},{24,16},{1,9},{9,1},{17,25},{25,17},{2,10},{10... | collective-permute-start | bytes 3145736 | tf_op jit(solution)/shard_map/ppermute | solution.py:21
  103.5 14.3 %collective-permute-start.22 = (bf16[2,128,1024]{2,1,0:T(8,128)(2,1)S(1)}, bf16[2,128,1024]{2,1,0:T(8,128)(2,1)S(1)}, u32[]{:S(2)}, u32[]{:S(2)}) collective-permute-start(bf16[2,128,1024]{2,1,0:T(8,128)(2,1)S(1)} %copy-done.16), channel_id=1, source_target_pairs={{0,2},{1,3},{2,0},{3,1},{4,6},{5,7},{6,4},{7,5},{8,10},{9,11},{10,... | collective-permute-start | bytes 1572872 | tf_op jit(solution)/shard_map/ppermute | solution.py:21
  104.6 13.2 %copy-start.15 = (bf16[2,128,1024]{2,1,0:T(8,128)(2,1)S(1)}, bf16[2,128,1024]{2,1,0:T(8,128)(2,1)}, u32[]{:S(2)}) copy-start(bf16[2,128,1024]{2,1,0:T(8,128)(2,1)} %get-tuple-element.21) | copy-start | bytes 1572868
  104.6 14.3 %copy-start.11 = (f32[2,128,1024]{2,1,0:T(8,128)S(1)}, f32[2,128,1024]{2,1,0:T(8,128)}, u32[]{:S(2)}) copy-start(f32[2,128,1024]{2,1,0:T(8,128)} %get-tuple-element.23) | copy-start | bytes 3145732
  106.0 13.1 %copy-start.5 = (f32[2,128,1024]{2,1,0:T(8,128)}, f32[2,128,1024]{2,1,0:T(8,128)S(1)}, u32[]{:S(2)}) copy-start(f32[2,128,1024]{2,1,0:T(8,128)S(1)} %convert_add_fusion) | copy-start | bytes 3145732
  106.0 25.6 %collective-permute-start.7 = (bf16[2,128,1024]{2,1,0:T(8,128)(2,1)}, bf16[2,128,1024]{2,1,0:T(8,128)(2,1)S(1)}, u32[]{:S(2)}, u32[]{:S(2)}) collective-permute-start(bf16[2,128,1024]{2,1,0:T(8,128)(2,1)} %collective-permute-done.6), channel_id=1, source_target_pairs={{0,1},{1,0},{2,3},{3,2},{4,5},{5,4},{6,7},{7,6},{8,9},{9,8},{10,11... | collective-permute-start | bytes 1572872 | tf_op jit(solution)/shard_map/ppermute | solution.py:21
  107.1 24.1 %copy-start.10 = (f32[2,128,1024]{2,1,0:T(8,128)S(1)}, f32[2,128,1024]{2,1,0:T(8,128)}, u32[]{:S(2)}) copy-start(f32[2,128,1024]{2,1,0:T(8,128)} %get-tuple-element.20) | copy-start | bytes 3145732
  117.8 13.4 %collective-permute-start.19 = (bf16[2,128,1024]{2,1,0:T(8,128)(2,1)S(1)}, bf16[2,128,1024]{2,1,0:T(8,128)(2,1)S(1)}, u32[]{:S(2)}, u32[]{:S(2)}) collective-permute-start(bf16[2,128,1024]{2,1,0:T(8,128)(2,1)S(1)} %copy-done.15), channel_id=1, source_target_pairs={{0,2},{1,3},{2,0},{3,1},{4,6},{5,7},{6,4},{7,5},{8,10},{9,11},{10,... | collective-permute-start | bytes 1572872 | tf_op jit(solution)/shard_map/ppermute | solution.py:21
  119.1 16.0 %copy-start.6 = (f32[2,128,1024]{2,1,0:T(8,128)}, f32[2,128,1024]{2,1,0:T(8,128)S(1)}, u32[]{:S(2)}) copy-start(f32[2,128,1024]{2,1,0:T(8,128)S(1)} %convert_add_fusion.2) | copy-start | bytes 3145732
  131.2 4.7 %collective-permute-start.3 = (bf16[2,8,4,32,128]{4,3,2,1,0:T(8,128)(2,1)S(1)}, bf16[2,8,4,32,128]{4,3,2,1,0:T(8,128)(2,1)S(1)}, u32[]{:S(2)}, u32[]{:S(2)}) collective-permute-start(bf16[2,8,4,32,128]{4,3,2,1,0:T(8,128)(2,1)S(1)} %pad_maximum_fusion.2), channel_id=1, source_target_pairs={{0,8},{8,0},{16,24},{24,16},{1,9},{9,1},{17,25},{25,17},{2,10},{10... | collective-permute-start | bytes 1572872 | tf_op jit(solution)/shard_map/ppermute | solution.py:21
  131.4 27.3 %collective-permute-start.29 = (bf16[1,128,1024]{2,1,0:T(8,128)(2,1)}, bf16[1,128,1024]{2,1,0:T(8,128)(2,1)}, u32[]{:S(2)}, u32[]{:S(2)}) collective-permute-start(bf16[1,128,1024]{2,1,0:T(8,128)(2,1)} %dynamic-slice_convert_fusion), channel_id=1, source_target_pairs={{0,4},{1,5},{2,6},{3,7},{4,0},{5,1},{6,2},{7,3},{8,12},{9,13},{10,... | collective-permute-start | bytes 786440 | tf_op jit(solution)/shard_map/ppermute | solution.py:21
  131.6 4.2 %copy-start.12 = (bf16[2,128,1024]{2,1,0:T(8,128)(2,1)}, bf16[2,128,1024]{2,1,0:T(8,128)(2,1)S(1)}, u32[]{:S(2)}) copy-start(bf16[2,128,1024]{2,1,0:T(8,128)(2,1)S(1)} %collective-permute-done.7.refs_1_) | copy-start | bytes 1572868
  131.6 32.7 %collective-permute-start.26 = (bf16[1,128,1024]{2,1,0:T(8,128)(2,1)}, bf16[1,128,1024]{2,1,0:T(8,128)(2,1)}, u32[]{:S(2)}, u32[]{:S(2)}) collective-permute-start(bf16[1,128,1024]{2,1,0:T(8,128)(2,1)} %dynamic-slice_convert_fusion.1), channel_id=1, source_target_pairs={{0,4},{1,5},{2,6},{3,7},{4,0},{5,1},{6,2},{7,3},{8,12},{9,13},{10,... | collective-permute-start | bytes 786440 | tf_op jit(solution)/shard_map/ppermute | solution.py:21
  135.9 33.6 %collective-permute-start.23 = (bf16[1,128,1024]{2,1,0:T(8,128)(2,1)}, bf16[1,128,1024]{2,1,0:T(8,128)(2,1)}, u32[]{:S(2)}, u32[]{:S(2)}) collective-permute-start(bf16[1,128,1024]{2,1,0:T(8,128)(2,1)} %dynamic-slice_convert_fusion.2), channel_id=1, source_target_pairs={{0,4},{1,5},{2,6},{3,7},{4,0},{5,1},{6,2},{7,3},{8,12},{9,13},{10,... | collective-permute-start | bytes 786440 | tf_op jit(solution)/shard_map/ppermute | solution.py:21
  143.0 27.5 %copy-start.7 = (f32[2,128,1024]{2,1,0:T(8,128)S(1)}, f32[2,128,1024]{2,1,0:T(8,128)}, u32[]{:S(2)}) copy-start(f32[2,128,1024]{2,1,0:T(8,128)} %copy-done.6) | copy-start | bytes 3145732
  158.7 15.1 %collective-permute-start.8 = (bf16[2,128,1024]{2,1,0:T(8,128)(2,1)}, bf16[2,128,1024]{2,1,0:T(8,128)(2,1)}, u32[]{:S(2)}, u32[]{:S(2)}) collective-permute-start(bf16[2,128,1024]{2,1,0:T(8,128)(2,1)} %collective-permute-done.5.refs_0_), channel_id=1, source_target_pairs={{0,16},{8,24},{16,0},{24,8},{1,17},{9,25},{17,1},{25,9},{2,18},{10... | collective-permute-start | bytes 1572872 | tf_op jit(solution)/shard_map/ppermute | solution.py:21
  164.3 19.0 %collective-permute-start.9 = (bf16[2,128,1024]{2,1,0:T(8,128)(2,1)}, bf16[2,128,1024]{2,1,0:T(8,128)(2,1)}, u32[]{:S(2)}, u32[]{:S(2)}) collective-permute-start(bf16[2,128,1024]{2,1,0:T(8,128)(2,1)} %copy-done.12), channel_id=1, source_target_pairs={{0,16},{8,24},{16,0},{24,8},{1,17},{9,25},{17,1},{25,9},{2,18},{10... | collective-permute-start | bytes 1572872 | tf_op jit(solution)/shard_map/ppermute | solution.py:21
  165.8 18.0 %copy-start.3 = (f32[1,512,1024]{2,1,0:T(8,128)S(1)}, f32[1,512,1024]{2,1,0:T(8,128)}, u32[]{:S(2)}) copy-start(f32[1,512,1024]{2,1,0:T(8,128)} %reshape.155) | copy-start | bytes 6291460
  167.2 16.7 %copy-start.2 = (f32[1,512,1024]{2,1,0:T(8,128)S(1)}, f32[1,512,1024]{2,1,0:T(8,128)}, u32[]{:S(2)}) copy-start(f32[1,512,1024]{2,1,0:T(8,128)} %param.8) | copy-start | bytes 6291460
  169.5 13.6 %collective-permute-start.20 = (bf16[1,128,1024]{2,1,0:T(8,128)(2,1)}, bf16[1,128,1024]{2,1,0:T(8,128)(2,1)S(1)}, u32[]{:S(2)}, u32[]{:S(2)}) collective-permute-start(bf16[1,128,1024]{2,1,0:T(8,128)(2,1)} %dynamic-slice_convert_fusion.3), channel_id=1, source_target_pairs={{0,4},{1,5},{2,6},{3,7},{4,0},{5,1},{6,2},{7,3},{8,12},{9,13},{10,... | collective-permute-start | bytes 786440 | tf_op jit(solution)/shard_map/ppermute | solution.py:21
  169.5 16.4 %collective-permute-start.16 = (bf16[4,128,1024]{2,1,0:T(8,128)(2,1)}, bf16[4,128,1024]{2,1,0:T(8,128)(2,1)}, u32[]{:S(2)}, u32[]{:S(2)}) collective-permute-start(bf16[4,128,1024]{2,1,0:T(8,128)(2,1)} %collective-permute-done.14.refs_1_), channel_id=1, source_target_pairs={{0,8},{8,0},{16,24},{24,16},{1,9},{9,1},{17,25},{25,17},{2,10},{10... | collective-permute-start | bytes 3145736 | tf_op jit(solution)/shard_map/ppermute | solution.py:21
  173.8 19.1 %collective-permute-start.10 = (bf16[2,128,1024]{2,1,0:T(8,128)(2,1)}, bf16[2,128,1024]{2,1,0:T(8,128)(2,1)}, u32[]{:S(2)}, u32[]{:S(2)}) collective-permute-start(bf16[2,128,1024]{2,1,0:T(8,128)(2,1)} %collective-permute-done.5.refs_0_), channel_id=1, source_target_pairs={{0,8},{8,0},{16,24},{24,16},{1,9},{9,1},{17,25},{25,17},{2,10},{10... | collective-permute-start | bytes 1572872 | tf_op jit(solution)/shard_map/ppermute | solution.py:21
  183.0 9.9 %collective-permute-start.11 = (bf16[2,128,1024]{2,1,0:T(8,128)(2,1)}, bf16[2,128,1024]{2,1,0:T(8,128)(2,1)}, u32[]{:S(2)}, u32[]{:S(2)}) collective-permute-start(bf16[2,128,1024]{2,1,0:T(8,128)(2,1)} %copy-done.12), channel_id=1, source_target_pairs={{0,8},{8,0},{16,24},{24,16},{1,9},{9,1},{17,25},{25,17},{2,10},{10... | collective-permute-start | bytes 1572872 | tf_op jit(solution)/shard_map/ppermute | solution.py:21
  183.3 9.7 %collective-permute-start.12 = (bf16[2,128,1024]{2,1,0:T(8,128)(2,1)}, bf16[2,128,1024]{2,1,0:T(8,128)(2,1)}, u32[]{:S(2)}, u32[]{:S(2)}) collective-permute-start(bf16[2,128,1024]{2,1,0:T(8,128)(2,1)} %collective-permute-done.8.refs_2_), channel_id=1, source_target_pairs={{0,8},{8,0},{16,24},{24,16},{1,9},{9,1},{17,25},{25,17},{2,10},{10... | collective-permute-start | bytes 1572872 | tf_op jit(solution)/shard_map/ppermute | solution.py:21
  183.5 9.4 %collective-permute-start.13 = (bf16[2,128,1024]{2,1,0:T(8,128)(2,1)}, bf16[2,128,1024]{2,1,0:T(8,128)(2,1)S(1)}, u32[]{:S(2)}, u32[]{:S(2)}) collective-permute-start(bf16[2,128,1024]{2,1,0:T(8,128)(2,1)} %collective-permute-done.9.refs_3_), channel_id=1, source_target_pairs={{0,8},{8,0},{16,24},{24,16},{1,9},{9,1},{17,25},{25,17},{2,10},{10... | collective-permute-start | bytes 1572872 | tf_op jit(solution)/shard_map/ppermute | solution.py:21
  (2 other events, 1.8 us)

commit v2 on v1

--- a/solution.py
+++ b/solution.py
@@ -36,33 +36,26 @@
     return out
 
 
-def dot_t(left, right):
-    return lax.dot_general(left, right, (((0,), (0,)), ((), ())), preferred_element_type=jnp.float32)
-
-
-def take_halves(place, x, rows_dev, chunks, first, count):
+def take_halves(place, x, rows_dev, chunks):
     tokens, feat = x.shape
     halves = feat // rows_dev // 2
     rows = rows_dev // chunks
 
-    def column(k):
-        return lambda h, p: (0, (2 * h + 1 - p[0]) * chunks + k)
-
-    def body(place_ref, *refs):
-        for k in range(count):
-            refs[count + k][...] = refs[k][...]
+    def body(p, xb, *outs):
+        for k in range(chunks):
+            outs[k][...] = xb[:, k * rows : (k + 1) * rows]
 
     return pl.pallas_call(
         body,
         grid_spec=pltpu.PrefetchScalarGridSpec(
             num_scalar_prefetch=1,
             grid=(halves,),
-            in_specs=[pl.BlockSpec((tokens, rows), column(first + k)) for k in range(count)],
-            out_specs=[pl.BlockSpec((tokens, rows), lambda h, p: (0, h)) for _ in range(count)],
+            in_specs=[pl.BlockSpec((tokens, rows_dev), lambda h, p: (0, 2 * h + 1 - p[0]))],
+            out_specs=[pl.BlockSpec((tokens, rows), lambda h, p: (0, h)) for _ in range(chunks)],
         ),
-        out_shape=[jax.ShapeDtypeStruct((tokens, halves * rows), x.dtype) for _ in range(count)],
+        out_shape=[jax.ShapeDtypeStruct((tokens, halves * rows), x.dtype) for _ in range(chunks)],
         name="take_halves",
-    )(place, *([x] * count))
+    )(place, x)
 
 
 def pair_dot(place, x_own, x_recv, dy_own, dy_recv, chunk, chunks, halves):
@@ -80,15 +73,21 @@
         return pl.BlockSpec((tokens, rows), at)
 
     def body(p, *refs):
-        owns, (xr, do, dr, send, keep) = refs[: 2 * quarter], refs[2 * quarter :]
-        recvs = []
-        for mine in (False, True):
-            for i in range(quarter):
-                half = 2 * i + (p[1] if mine else 1 - p[1])
-                recvs.append(xr[:, pl.ds(pl.multiple_of(half * rows, rows), rows)])
-        own = jnp.concatenate([r[...] for r in owns], axis=1)
-        recv = jnp.concatenate(recvs, axis=1)
-        total = dot_t(own, do[...]) + dot_t(recv, dr[...])
+        owns, (xr, do, dr, send, keep, own, recv) = refs[: 2 * quarter], refs[2 * quarter :]
+
+        @pl.when(pl.program_id(0) == 0)
+        def _():
+            n = 0
+            for mine in (False, True):
+                for i in range(quarter):
+                    half = 2 * i + (p[1] if mine else 1 - p[1])
+                    at = slice(n * rows, (n + 1) * rows)
+                    own[at] = owns[n][...].T
+                    recv[at] = xr[:, pl.ds(pl.multiple_of(half * rows, rows), rows)].T
+                    n += 1
+
+        total = jnp.dot(own[...], do[...], preferred_element_type=jnp.float32)
+        total = total + jnp.dot(recv[...], dr[...], preferred_element_type=jnp.float32)
         total = total.reshape(2, quarter, rows, columns)
         send[...] = total[0].astype(send.dtype)
         keep[...] = total[1]
@@ -105,6 +104,7 @@
                 pl.BlockSpec((tokens, columns), lambda c, p: (0, c)),
             ],
             out_specs=[pl.BlockSpec((quarter, rows, columns), lambda c, p: (0, 0, c))] * 2,
+            scratch_shapes=[pltpu.VMEM((2 * quarter * rows, tokens), jnp.bfloat16)] * 2,
         ),
         out_shape=[
             jax.ShapeDtypeStruct((quarter, rows, width), jnp.bfloat16),
@@ -158,45 +158,80 @@
     )(place, index, x, dy)
 
 
+def block_onehot(ix, own_rows, tiles_row, live=None):
+    slots = ix.shape[1]
+    kind = jnp.bfloat16 if own_rows <= 256 else jnp.float32
+    q = lax.broadcasted_iota(jnp.int32, (own_rows, slots), 0).astype(jnp.float32).astype(kind)
+    named = ix >= 0 if live is None else jnp.logical_and(ix >= 0, live)
+    row = jnp.maximum(ix, 0) // tiles_row
+    column = jnp.maximum(ix, 0) - row * tiles_row
+    out = []
+    for c in range(tiles_row):
+        at = jnp.where(jnp.logical_and(named, column == c), row, -1).astype(jnp.float32).astype(kind)
+        out.append(jnp.where(q == at, jnp.ones((), kind), jnp.zeros((), kind)).astype(jnp.bfloat16))
+    return jnp.concatenate(out, axis=0)
+
+
 def block_delta(ix, values, own_rows, tiles_row):
-    slots = ix.shape[1]
-    q = lax.broadcasted_iota(jnp.int32, (own_rows, slots), 0) * tiles_row
-    onehot = [jnp.where(q == ix - c, 1.0, 0.0).astype(jnp.bfloat16) for c in range(tiles_row)]
-    return jnp.dot(jnp.concatenate(onehot, axis=0), values, preferred_element_type=jnp.float32)
-
-
-def momentum_step(place, momentum, index, values):
-    rows_dev, width = momentum.shape
-    islands, _, owners, cap, _ = values.shape
-    own_rows = rows_dev // owners
+    return jnp.dot(block_onehot(ix, own_rows, tiles_row), values, preferred_element_type=jnp.float32)
+
+
+def error_step(place, parts, first, index, error, own_rows, scale, before):
+    rows_dev, width = error.shape
+    count, each = len(parts), len(parts[0])
+    rows = parts[0][0].shape[1]
+    group = 4 * parts[0][0].shape[0]
     tiles_row = width // TILE
-    slots = islands * cap
-
-    def body(p, ix, v, mom, out):
-        parts = block_delta(ix[0, 0], v[...].reshape(slots, TILE), own_rows, tiles_row)
-        for c in range(tiles_row):
-            at = slice(c * TILE, (c + 1) * TILE)
-            part = parts[c * own_rows : (c + 1) * own_rows]
-            out[:, at] = outer_momentum * mom[:, at] + part * (1.0 / islands)
-
+    owners = rows_dev // own_rows
+    slots = index.shape[1]
+    cap = slots // owners
+    flat = [a for part in parts for a in part]
+
+    def body(p, ix, err, *refs):
+        out = refs[-1]
+        lane = lax.broadcasted_iota(jnp.int32, (1, slots), 1) // cap
+        for s in range(count):
+
+            @pl.when(pl.program_id(0) == s)
+            def _(s=s):
+                terms = refs[s * each : (s + 1) * each]
+                for n in range(rows // own_rows):
+                    owner = (first + s) * (rows // own_rows) + n
+                    onehot = block_onehot(ix[...], own_rows, tiles_row, lane == owner)
+                    hits = jnp.dot(onehot, jnp.ones((slots, TILE), jnp.bfloat16), preferred_element_type=jnp.float32)
+                    to = slice(n * own_rows, (n + 1) * own_rows)
+                    for c in range(tiles_row):
+                        at = slice(c * TILE, (c + 1) * TILE)
+                        grad = terms[0][0, to, at]
+                        for term in terms[1:]:
+                            grad = grad + term[0, to, at].astype(jnp.float32)
+                        value = feedback_decay * err[to, at] + scale * grad
+                        out[to, at] = jnp.where(hits[c * own_rows : (c + 1) * own_rows] > 0.0, 0.0, value)
+
+    def own_block(a):
+        shift = (group // a.shape[0]).bit_length() - 1
+        return pl.BlockSpec((1, rows, width), lambda g, p: (p[2] >> shift, 0, 0))
+
+    extra = [] if before is None else [before]
+    block = pl.BlockSpec((rows, width), lambda g, p: (first + g, 0))
     return pl.pallas_call(
         body,
         grid_spec=pltpu.PrefetchScalarGridSpec(
             num_scalar_prefetch=1,
-            grid=(owners,),
+            grid=(count,),
             in_specs=[
-                pl.BlockSpec((1, 1, 1, slots), lambda o, p: (p[2], o, 0, 0)),
-                pl.BlockSpec((islands, 1, 1, cap, TILE), lambda o, p: (0, p[2], o, 0, 0)),
-                pl.BlockSpec((own_rows, width), lambda o, p: (o, 0)),
+                pl.BlockSpec(index.shape, lambda g, p: (0, 0)), block, *[own_block(a) for a in flat],
+                *[pl.BlockSpec(memory_space=pl.ANY) for _ in extra],
             ],
-            out_specs=pl.BlockSpec((own_rows, width), lambda o, p: (o, 0)),
+            out_specs=block,
         ),
-        out_shape=jax.ShapeDtypeStruct(momentum.shape, jnp.float32),
-        name="momentum_step",
-    )(place, index, values, momentum)
-
-
-def weight_step(sets, groups, where, index, values, shape, before=None):
+        out_shape=jax.ShapeDtypeStruct(error.shape, jnp.float32),
+        input_output_aliases={} if before is None else {3 + len(flat): 0},
+        name="error_step",
+    )(place, index, error, *flat, *extra)
+
+
+def weight_step(sets, groups, where, index, values, shape, momentum=None, before=None):
     count, subs = len(sets), len(sets[0])
     per = sets[0][0].shape[0]
     pieces = subs * per
@@ -208,7 +243,8 @@
     flat = [a for one in sets for a in one]
 
     def body(w, ix, v, *refs):
-        arrays, (out, held, sems) = refs[: len(flat)], refs[-3:]
+        arrays, (held, sems) = refs[: len(flat)], refs[-2:]
+        out = refs[-3] if momentum is None else refs[-4]
         step = pl.program_id(0)
 
         def copy(n):
@@ -235,9 +271,15 @@
             for c in range(tiles_row):
                 at = slice(c * TILE, (c + 1) * TILE)
                 part = parts[c * own_rows : (c + 1) * own_rows]
+                if momentum is not None and groups[i] == 0:
+                    refs[-3][:, at] = outer_momentum * refs[len(flat)][:, at] + part * (1.0 / islands)
                 out[to, 0, 0, :, at] = (held[step, i, :, at].astype(jnp.float32) - rate * part).astype(jnp.bfloat16)
 
-    extra = [] if before is None else [before]
+    extra = [v for v in (momentum, before) if v is not None]
+    rows = pl.BlockSpec((own_rows, width), lambda g, w: (w[2 + g], 0))
+    hbm = pl.BlockSpec(memory_space=pl.ANY)
+    new_weight = jax.ShapeDtypeStruct(shape, jnp.bfloat16)
+    block = pl.BlockSpec((halves, 1, 1, own_rows, width), lambda g, w: (0, w[0], w[2 + g], 0, 0))
     return pl.pallas_call(
         body,
         grid_spec=pltpu.PrefetchScalarGridSpec(
@@ -246,16 +288,18 @@
             in_specs=[
                 pl.BlockSpec(index.shape, lambda g, w: (0, 0, 0, 0)),
                 pl.BlockSpec(values.shape, lambda g, w: (0, 0, 0, 0, 0)),
-                *[pl.BlockSpec(memory_space=pl.ANY) for _ in flat + extra],
+                *[hbm for _ in flat],
+                *([] if momentum is None else [rows]),
+                *([] if before is None else [hbm]),
             ],
-            out_specs=pl.BlockSpec((halves, 1, 1, own_rows, width), lambda g, w: (0, w[0], w[2 + g], 0, 0)),
+            out_specs=block if momentum is None else [block, rows],
             scratch_shapes=[
                 pltpu.VMEM((count, pieces, own_rows, width), jnp.bfloat16),
                 pltpu.SemaphoreType.DMA((len(flat),)),
             ],
         ),
-        out_shape=jax.ShapeDtypeStruct(shape, jnp.bfloat16),
-        input_output_aliases={} if before is None else {3 + len(flat): 0},
+        out_shape=new_weight if momentum is None else [new_weight, jax.ShapeDtypeStruct(momentum.shape, jnp.float32)],
+        input_output_aliases={} if before is None else {2 + len(flat) + len(extra): 0},
         name="weight_step",
     )(where, index, values, *flat, *extra)
 
@@ -284,12 +328,10 @@
     island_numbers = numbers.reshape(group, 1, islands * cap)
 
     dy_recv = swap(grad_out, "inside", 0)
-    x_send = take_halves(place, inputs, rows_dev, chunks, 0, 1)
-    if chunks > 1:
-        x_send += take_halves(place, inputs, rows_dev, chunks, 1, chunks - 1)
+    x_send = take_halves(place, inputs, rows_dev, chunks)
 
     terms = slot_terms(place, inputs, grad_out, island_numbers, rows_dev, own_rows)
-    index, terms, numbers = lax.optimization_barrier((index, terms, numbers))
+    terms, numbers = lax.optimization_barrier((terms, numbers))
     terms = lax.all_to_all(terms, "inside", split_axis=0, concat_axis=0, tiled=True)
 
     numbers = numbers[None]
@@ -333,33 +375,31 @@
         far_sets += swap_sets(far_sets, bit)
         owners += [o ^ (1 << bit) for o in owners]
     set_owner = [b ^ o for o in owners]
-    new_weight = None
-    for parity, sets in enumerate((near_sets, far_sets)):
-        gone = [g ^ parity for g in base_group]
-        where = jnp.stack([(j & 1) ^ parity, j, *set_owner])
-        new_weight = weight_step(
-            sets, gone, where, by_device, values,
-            (halves, 2, islands, own_rows, width), new_weight,
-        )
+    shape = (halves, 2, islands, own_rows, width)
+    where = [jnp.stack([(j & 1) ^ parity, j, *set_owner]) for parity in range(2)]
+    new_weight, new_momentum = weight_step(near_sets, base_group, where[0], by_device, values, shape, momentum)
+    new_weight = weight_step(far_sets, [g ^ 1 for g in base_group], where[1], by_device, values, shape, None, new_weight)
     new_weight = new_weight.reshape(feat, width)
-    new_momentum = momentum_step(place, momentum, by_device, values)
-
-    hit = jnp.any(index[:, None, None, :] == jnp.arange(own_tiles, dtype=jnp.int32).reshape(1, own_rows, tiles_row, 1), axis=3)
-    free = jnp.where(hit.reshape(rows_dev, tiles_row, 1), 0.0, 1.0)
-    free = jnp.broadcast_to(free, (rows_dev, tiles_row, TILE)).reshape(rows_dev, width)
+
     parts = []
     for k in range(chunks):
         send, keep = pair_dot(place, inputs, x_recv[k], grad_out, dy_recv, k, chunks, halves)
-        current = keep + swap(send, "inside", 1).astype(jnp.float32)
+        recv = swap(send, "inside", 1)
+        terms = [keep, recv]
         for bit in range(2, inside_bits):
+            current = (keep + recv.astype(jnp.float32)).reshape(keep.shape[0] // 2, 2, rows, width)
             mine = (j >> bit) & 1
-            current = current.reshape(current.shape[0] // 2, 2, rows, width)
             send = lax.dynamic_index_in_dim(current, 1 - mine, 1, keepdims=False).astype(jnp.bfloat16)
             keep = lax.dynamic_index_in_dim(current, mine, 1, keepdims=False)
-            current = keep + swap(send, "inside", bit).astype(jnp.float32)
-        parts.append(current[0])
-    grad = jnp.concatenate(parts, axis=0)
-    new_error = (free * (feedback_decay * error[0] + scale * grad))[None]
+            recv = swap(send, "inside", bit)
+            terms.append(recv)
+        parts.append(terms)
+    flat_index = index.reshape(1, islands * cap)
+    new_error = None
+    for first, some in ((0, parts[:-1]), (chunks - 1, parts[-1:])):
+        if some:
+            new_error = error_step(place, some, first, flat_index, error[0], own_rows, scale, new_error)
+    new_error = new_error[None]
     return (new_weight, new_momentum, new_error)
 
 

time: 202 us -> 228 us (1.13)
  waiting for transfers between devices: 69.5 us -> 99.1 us
  local copies, waits for them, and re-layouts: 16.4 us -> 12.3 us
  Pallas kernels: 53.4 us -> 55.7 us
  other arithmetic: 17.2 us -> 14.9 us
    all_to_all x1, waiting for transfers between devices: 0.01 us -> 26 us  [local(): lax.all_to_all(terms, 'inside', split_axis=0, concat_axis=0, tiled=True)]
    ppermute x30, waiting for transfers between devices: 55.5 us -> 69.4 us  [swap(): return lax.ppermute(values, axis, [(i, i ^ 1 << bit) for i in range(size)])]
    all_to_all x2, waiting for transfers between devices: 14 us -> 3.74 us  [spread(): lax.all_to_all(every, 'inside', split_axis=0, concat_axis=0, tiled=True)]
    add x8 -> x0, other arithmetic: 5.29 us -> none  [the longest x4 3.41 us: local(): current = keep + swap(send, 'inside', bit).astype(jnp.float32)]
    convert_element_type x0 -> x4, other arithmetic: none -> 4.23 us  [local(): lax.dynamic_index_in_dim(current, 1 - mine, 1, keepdims=False)]
    pallas_call x2 -> x1, Pallas kernels: 8.31 us -> 4.68 us  [take_halves(): pl.pallas_call(body, grid_spec=pltpu.PrefetchScalarGridSpec(num_scalar_pr...]
    pallas_call x1 -> x2, Pallas kernels: 4.9 us -> 8.36 us  [error_step(): pl.pallas_call(body, grid_spec=pltpu.PrefetchScalarGridSpec(num_scalar_pr...]
    convert_element_type x4 -> x0, local copies, waits for them, and re-layouts: 3.09 us -> none  [local(): lax.dynamic_index_in_dim(current, 1 - mine, 1, keepdims=False)]
  transfers between devices with their start and end apart: 33 -> 33, of which waited for: 11 -> 10; matrix products, arithmetic and copies ran while one was open for 15% -> 10% of each run, Pallas kernels for 23% -> 21%
where the time goes in v2:
time: 228 us; the launch traced here: 227 us
  waiting for transfers between devices  99.1 us (43%)
  Pallas kernels  55.7 us (24%)
  starting transfers between devices  43.7 us (19%)
  other arithmetic  14.9 us (7%)
  local copies, waits for them, and re-layouts  12.3 us (5%)
    ppermute x30, waiting for transfers between devices, swap(): return lax.ppermute(values, axis, [(i, i ^ 1 << bit) for i in range(size)])  69.4 us
    ppermute x30, starting transfers between devices, swap(): return lax.ppermute(values, axis, [(i, i ^ 1 << bit) for i in range(size)])  28.8 us
    all_to_all x1, waiting for transfers between devices, local(): lax.all_to_all(terms, 'inside', split_axis=0, concat_axis=0, tiled=True)  26 us
    pallas_call x4, Pallas kernels, pair_dot(): pl.pallas_call(body, grid_spec=pltpu.PrefetchScalarGridSpec(num_scalar_pr...  19.8 us
    pallas_call x2, Pallas kernels, weight_step(): pl.pallas_call(body, grid_spec=pltpu.PrefetchScalarGridSpec(num_scalar_pr...  15.4 us
    all_to_all x2, starting transfers between devices, spread(): lax.all_to_all(every, 'inside', split_axis=0, concat_axis=0, tiled=True)  10.9 us
    pallas_call x2, Pallas kernels, error_step(): pl.pallas_call(body, grid_spec=pltpu.PrefetchScalarGridSpec(num_scalar_pr...  8.36 us
    pallas_call x1, Pallas kernels, slot_terms(): pl.pallas_call(body, grid_spec=pltpu.PrefetchScalarGridSpec(num_scalar_pr...  7.44 us
  transfers between devices with their start and end apart: 33, of which 10 were waited for; matrix products, arithmetic and copies ran while one was open for 10% of the time, Pallas kernels for 21%

profile of v2, /device:TPU:0, one launch (start us, length us, event | category | flops | bytes accessed | tf_op | source)
XLA Modules:
  0.0 226.7 jit_solution(5504631376020365729)
XLA Ops:
  2.0 7.3 %all-to-all-start = ((s32[8,1,128]{2,1,0:T(1,128)}), s32[8,1,128]{2,1,0:T(1,128)S(1)}, u32[]{:S(2)}, u32[]{:S(2)}) async-start(s32[8,1,128]{2,1,0:T(1,128)} %reshape.93), calls=%async_computation | async-start | bytes 8192 | tf_op jit(solution)/shard_map/all_to_all | solution.py:27
  9.3 1.9 fusion.4
  11.2 2.9 %collective-permute-start.4 = (bf16[1,128,1024]{2,1,0:T(8,128)(2,1)}, bf16[1,128,1024]{2,1,0:T(8,128)(2,1)}, u32[]{:S(2)}, u32[]{:S(2)}) collective-permute-start(bf16[1,128,1024]{2,1,0:T(8,128)(2,1)} %fusion.4), channel_id=1, source_target_pairs={{0,4},{1,5},{2,6},{3,7},{4,0},{5,1},{6,2},{7,3},{8,12},{9,13},{10,... | collective-permute-start | bytes 786440 | tf_op jit(solution)/shard_map/ppermute | solution.py:21
  14.7 4.7 %take_halves.1 = (bf16[512,512]{1,0:T(8,128)(2,1)}, bf16[512,512]{1,0:T(8,128)(2,1)}, bf16[512,512]{1,0:T(8,128)(2,1)}, bf16[512,512]{1,0:T(8,128)(2,1)}) custom-call(s32[3]{0:T(128)} %pad_add_fusion.1.p, bf16[512,4096]{1,0:T(8,128)(2,1)} %refs_3_.7), custom_call_target="tpu_custom_call" | custom-call | tf_op jit(solution)/shard_map/take_halves/pallas_call | solution.py:48
  19.4 1.5 collective-permute-start.17
  21.5 1.5 collective-permute-start.21
  24.9 7.4 %slot_terms.1 = bf16[8,128,128]{2,1,0:T(8,128)(2,1)} custom-call(s32[3]{0:T(128)} %pad_add_fusion.1.p, s32[8,1,128]{2,1,0:T(1,128)} %reshape.79.ix, bf16[512,4096]{1,0:T(8,128)(2,1)} %refs_3_.7, bf16[512,1024]{1,0:T(8,128)(2,1)} %refs_5_.7), custom_call_target="tpu_custom_call" | custom-call | tf_op jit(solution)/shard_map/slot_terms/pallas_call | solution.py:143
  32.3 4.1 %all-to-all-start.1 = ((bf16[8,128,128]{2,1,0:T(8,128)(2,1)}), bf16[8,128,128]{2,1,0:T(8,128)(2,1)}, u32[]{:S(2)}, u32[]{:S(2)}) async-start(bf16[8,128,128]{2,1,0:T(8,128)(2,1)} %slot_terms.1), calls=%async_computation.1 | async-start | bytes 524288 | tf_op jit(solution)/shard_map/all_to_all | solution.py:335
  36.4 1.5 reshape_squeeze.6
  38.0 2.6 %gather_fusion = f32[128,128]{1,0:T(8,128)S(1)} fusion(f32[4,1024,128]{2,1,0:T(8,128)} %reshape_squeeze.6, s32[128]{0:T(128)S(1)} %reshape.82), kind=kCustom, calls=%fused_computation | custom fusion | bytes 132096 | tf_op jit(solution)/shard_map/jit(take_along_axis)/gather | solution.py:361
  40.6 1.4 collective-permute-start
  41.9 1.1 pad_maximum_fusion.3
  43.0 2.0 collective-permute-start.5
  45.1 26.0 %all-to-all-done.1 = bf16[8,128,128]{2,1,0:T(8,128)(2,1)} async-done(((bf16[8,128,128]{2,1,0:T(8,128)(2,1)}), bf16[8,128,128]{2,1,0:T(8,128)(2,1)}, u32[]{:S(2)}, u32[]{:S(2)}) %all-to-all-start.1) | async-done | bytes 262176 | tf_op jit(solution)/shard_map/all_to_all | solution.py:335
  72.9 3.6 %all-to-all-start.2 = ((bf16[8,4,32,128]{3,2,1,0:T(8,128)(2,1)}), bf16[8,4,32,128]{3,2,1,0:T(8,128)(2,1)S(1)}, u32[]{:S(2)}, u32[]{:S(2)}) async-start(bf16[8,4,32,128]{3,2,1,0:T(8,128)(2,1)} %broadcast_in_dim.53), calls=%async_computation.2 | async-start | bytes 524288 | tf_op jit(solution)/shard_map/all_to_all | solution.py:27
  76.7 1.2 collective-permute-done.1
  77.9 2.0 collective-permute-start.6
  79.9 1.5 collective-permute-start.24
  81.9 3.7 %all-to-all-done.2 = bf16[8,4,32,128]{3,2,1,0:T(8,128)(2,1)S(1)} async-done(((bf16[8,4,32,128]{3,2,1,0:T(8,128)(2,1)}), bf16[8,4,32,128]{3,2,1,0:T(8,128)(2,1)S(1)}, u32[]{:S(2)}, u32[]{:S(2)}) %all-to-all-start.2) | async-done | bytes 262176 | tf_op jit(solution)/shard_map/all_to_all | solution.py:27
  85.7 1.5 collective-permute-start.2
  87.2 6.6 %collective-permute-done.6 = bf16[2,128,1024]{2,1,0:T(8,128)(2,1)} collective-permute-done((bf16[2,128,1024]{2,1,0:T(8,128)(2,1)S(1)}, bf16[2,128,1024]{2,1,0:T(8,128)(2,1)}, u32[]{:S(2)}, u32[]{:S(2)}) %collective-permute-start.6) | collective-permute-done | bytes 524320 | tf_op jit(solution)/shard_map/ppermute | solution.py:21
  93.8 1.6 collective-permute-start.7
  95.4 1.5 collective-permute-start.8
  96.9 1.3 pad_maximum_fusion.1.refs_0_
  98.2 4.9 %pair_dot.4 = (bf16[2,128,1024]{2,1,0:T(8,128)(2,1)}, f32[2,128,1024]{2,1,0:T(8,128)}) custom-call(s32[3]{0:T(128)} %pad_add_fusion.1.p, bf16[512,4096]{1,0:T(8,128)(2,1)} %refs_3_.7, bf16[512,4096]{1,0:T(8,128)(2,1)} %refs_3_.7, bf16[512,4096]{1,0:T(8,128)(2,1)} %refs_3_.7, bf16[512,4096]{1,0:T(8,128)(2,1)} %refs_3_.7, ...), custom_call_target="tpu_custom_call" | custom-call | tf_op jit(solution)/shard_map/pair_dot/pallas_call | solution.py:95
  103.1 4.9 %pair_dot.5 = (bf16[2,128,1024]{2,1,0:T(8,128)(2,1)}, f32[2,128,1024]{2,1,0:T(8,128)}) custom-call(s32[3]{0:T(128)} %pad_add_fusion.1.p, bf16[512,4096]{1,0:T(8,128)(2,1)} %refs_3_.7, bf16[512,4096]{1,0:T(8,128)(2,1)} %refs_3_.7, bf16[512,4096]{1,0:T(8,128)(2,1)} %refs_3_.7, bf16[512,4096]{1,0:T(8,128)(2,1)} %refs_3_.7, ...), custom_call_target="tpu_custom_call" | custom-call | tf_op jit(solution)/shard_map/pair_dot/pallas_call | solution.py:95
  109.0 1.6 collective-permute-start.22
  110.6 4.9 %pair_dot.6 = (bf16[2,128,1024]{2,1,0:T(8,128)(2,1)}, f32[2,128,1024]{2,1,0:T(8,128)}) custom-call(s32[3]{0:T(128)} %pad_add_fusion.1.p, bf16[512,4096]{1,0:T(8,128)(2,1)} %refs_3_.7, bf16[512,4096]{1,0:T(8,128)(2,1)} %refs_3_.7, bf16[512,4096]{1,0:T(8,128)(2,1)} %refs_3_.7, bf16[512,4096]{1,0:T(8,128)(2,1)} %refs_3_.7, bf16[512,512]{1,0:T(8,128)(2,1)} %copy-done.12, ...), custom_call_target="tpu_custom_call" | custom-call | tf_op jit(solution)/shard_map/pair_dot/pallas_call | solution.py:95
  115.6 5.1 %pair_dot.7 = (bf16[2,128,1024]{2,1,0:T(8,128)(2,1)}, f32[2,128,1024]{2,1,0:T(8,128)}) custom-call(s32[3]{0:T(128)} %pad_add_fusion.1.p, bf16[512,4096]{1,0:T(8,128)(2,1)} %refs_3_.7, bf16[512,4096]{1,0:T(8,128)(2,1)} %refs_3_.7, bf16[512,4096]{1,0:T(8,128)(2,1)} %refs_3_.7, bf16[512,4096]{1,0:T(8,128)(2,1)} %refs_3_.7, bf16[512,512]{1,0:T(8,128)(2,1)} %copy-done.13, ...), custom_call_target="tpu_custom_call" | custom-call | tf_op jit(solution)/shard_map/pair_dot/pallas_call | solution.py:95
  121.2 1.6 collective-permute-start.28
  122.8 1.8 pad_maximum_fusion.2
  124.6 10.3 %collective-permute-done.22.refs_1_ = bf16[2,128,1024]{2,1,0:T(8,128)(2,1)} collective-permute-done((bf16[2,128,1024]{2,1,0:T(8,128)(2,1)}, bf16[2,128,1024]{2,1,0:T(8,128)(2,1)}, u32[]{:S(2)}, u32[]{:S(2)}) %collective-permute-start.22) | collective-permute-done | bytes 524320 | tf_op jit(solution)/shard_map/ppermute | solution.py:21
  135.0 1.2 fusion.3
  136.1 1.0 fusion.2
  137.2 11.8 %collective-permute-done.25.refs_4_ = bf16[2,128,1024]{2,1,0:T(8,128)(2,1)} collective-permute-done((bf16[2,128,1024]{2,1,0:T(8,128)(2,1)}, bf16[2,128,1024]{2,1,0:T(8,128)(2,1)}, u32[]{:S(2)}, u32[]{:S(2)}) %collective-permute-start.25) | collective-permute-done | bytes 524320 | tf_op jit(solution)/shard_map/ppermute | solution.py:21
  149.3 11.6 %collective-permute-done.28.refs_7_ = bf16[2,128,1024]{2,1,0:T(8,128)(2,1)} collective-permute-done((bf16[2,128,1024]{2,1,0:T(8,128)(2,1)}, bf16[2,128,1024]{2,1,0:T(8,128)(2,1)}, u32[]{:S(2)}, u32[]{:S(2)}) %collective-permute-start.28) | collective-permute-done | bytes 524320 | tf_op jit(solution)/shard_map/ppermute | solution.py:21
  160.9 1.6 collective-permute-start.9
  162.5 1.0 fusion.1
  163.5 1.0 fusion
  164.6 3.0 %collective-permute-start.26 = (bf16[1,128,1024]{2,1,0:T(8,128)(2,1)S(1)}, bf16[1,128,1024]{2,1,0:T(8,128)(2,1)S(1)}, u32[]{:S(2)}, u32[]{:S(2)}) collective-permute-start(bf16[1,128,1024]{2,1,0:T(8,128)(2,1)S(1)} %fusion.1), channel_id=1, source_target_pairs={{0,4},{1,5},{2,6},{3,7},{4,0},{5,1},{6,2},{7,3},{8,12},{9,13},{10,... | collective-permute-start | bytes 786440 | tf_op jit(solution)/shard_map/ppermute | solution.py:21
  167.5 11.0 %collective-permute-done.23.refs_2_ = bf16[1,128,1024]{2,1,0:T(8,128)(2,1)S(1)} collective-permute-done((bf16[1,128,1024]{2,1,0:T(8,128)(2,1)S(1)}, bf16[1,128,1024]{2,1,0:T(8,128)(2,1)S(1)}, u32[]{:S(2)}, u32[]{:S(2)}) %collective-permute-start.23) | collective-permute-done | bytes 262176 | tf_op jit(solution)/shard_map/ppermute | solution.py:21
  178.6 11.2 %collective-permute-done.26.refs_5_ = bf16[1,128,1024]{2,1,0:T(8,128)(2,1)S(1)} collective-permute-done((bf16[1,128,1024]{2,1,0:T(8,128)(2,1)S(1)}, bf16[1,128,1024]{2,1,0:T(8,128)(2,1)S(1)}, u32[]{:S(2)}, u32[]{:S(2)}) %collective-permute-start.26) | collective-permute-done | bytes 262176 | tf_op jit(solution)/shard_map/ppermute | solution.py:21
  189.8 5.5 %collective-permute-done.29.refs_8_ = bf16[1,128,1024]{2,1,0:T(8,128)(2,1)S(1)} collective-permute-done((bf16[1,128,1024]{2,1,0:T(8,128)(2,1)S(1)}, bf16[1,128,1024]{2,1,0:T(8,128)(2,1)S(1)}, u32[]{:S(2)}, u32[]{:S(2)}) %collective-permute-start.29) | collective-permute-done | bytes 262176 | tf_op jit(solution)/shard_map/ppermute | solution.py:21
  198.9 2.1 pad_maximum_fusion.v
  201.0 5.3 %error_step.2.refs_3_ = f32[512,1024]{1,0:T(8,128)} custom-call(s32[3]{0:T(128)} %pad_add_fusion.1.p, s32[1,128]{1,0:T(1,128)} %reshape_squeeze.7.ix, f32[512,1024]{1,0:T(8,128)} %bitcast.26, f32[2,128,1024]{2,1,0:T(8,128)} %get-tuple-element.27.refs_0_, bf16[2,128,1024]{2,1,0:T(8,128)(2,1)} %collective-permute-done.22.refs_1_, ...), custom_call_target="tpu_custom_call" | custom-call | tf_op jit(solution)/shard_map/error_step/pallas_call | solution.py:217
  206.3 3.1 %error_step.3 = f32[512,1024]{1,0:T(8,128)} custom-call(s32[3]{0:T(128)} %pad_add_fusion.1.p, s32[1,128]{1,0:T(1,128)} %reshape_squeeze.7.ix, f32[512,1024]{1,0:T(8,128)} %bitcast.27, f32[2,128,1024]{2,1,0:T(8,128)} %get-tuple-element.24.refs_0_, bf16[2,128,1024]{2,1,0:T(8,128)(2,1)} %collective-permute-done.19.refs_1_, ...), custom_call_target="tpu_custom_call", output_to_operand_aliasing={{}: (6, {})} | custom-call | tf_op jit(solution)/shard_map/error_step/pallas_call | solution.py:217
  210.4 8.3 %weight_step.2 = (bf16[4,2,4,128,1024]{4,3,2,1,0:T(8,128)(2,1)}, f32[512,1024]{1,0:T(8,128)}) custom-call(s32[6]{0:T(128)} %stack.50.w, s32[8,4,1,128]{3,2,1,0:T(1,128)} %reshape.80.ix, bf16[4,8,4,32,128]{4,3,2,1,0:T(8,128)(2,1)} %pad_maximum_fusion.v, bf16[4,128,1024]{2,1,0:T(8,128)(2,1)} %copy-done.2, ...), custom_call_target="tpu_custom_call" | custom-call | tf_op jit(solution)/shard_map/weight_step/pallas_call | solution.py:283
  219.6 7.0 %weight_step.3 = bf16[4,2,4,128,1024]{4,3,2,1,0:T(8,128)(2,1)} custom-call(s32[6]{0:T(128)} %stack.46.w, s32[8,4,1,128]{3,2,1,0:T(1,128)} %reshape.80.ix, bf16[4,8,4,32,128]{4,3,2,1,0:T(8,128)(2,1)} %pad_maximum_fusion.v, bf16[2,128,1024]{2,1,0:T(8,128)(2,1)} %collective-permute-done.5.refs_0_, ...), custom_call_target="tpu_custom_call", output_to_operand_aliasing={{}: (11, {})} | custom-call | tf_op jit(solution)/shard_map/weight_step/pallas_call | solution.py:283
  (97 shorter events, 14.4 us)
Async XLA Ops:
  2.0 20.9 %all-to-all-start = ((s32[8,1,128]{2,1,0:T(1,128)}), s32[8,1,128]{2,1,0:T(1,128)S(1)}, u32[]{:S(2)}, u32[]{:S(2)}) async-start(s32[8,1,128]{2,1,0:T(1,128)} %reshape.93), calls=%async_computation | async-start | bytes 8192 | tf_op jit(solution)/shard_map/all_to_all | solution.py:27
  11.2 30.8 %collective-permute-start.4 = (bf16[1,128,1024]{2,1,0:T(8,128)(2,1)}, bf16[1,128,1024]{2,1,0:T(8,128)(2,1)}, u32[]{:S(2)}, u32[]{:S(2)}) collective-permute-start(bf16[1,128,1024]{2,1,0:T(8,128)(2,1)} %fusion.4), channel_id=1, source_target_pairs={{0,4},{1,5},{2,6},{3,7},{4,0},{5,1},{6,2},{7,3},{8,12},{9,13},{10,... | collective-permute-start | bytes 786440 | tf_op jit(solution)/shard_map/ppermute | solution.py:21
  14.7 6.1 %copy-start = (bf16[512,1024]{1,0:T(8,128)(2,1)S(1)}, bf16[512,1024]{1,0:T(8,128)(2,1)}, u32[]{:S(2)}) copy-start(bf16[512,1024]{1,0:T(8,128)(2,1)} %refs_5_.7) | copy-start | bytes 3145732
  19.4 60.5 %collective-permute-start.17 = (bf16[512,512]{1,0:T(8,128)(2,1)}, bf16[512,512]{1,0:T(8,128)(2,1)}, u32[]{:S(2)}, u32[]{:S(2)}) collective-permute-start(bf16[512,512]{1,0:T(8,128)(2,1)} %get-tuple-element.23), channel_id=1, source_target_pairs={{0,1},{1,0},{2,3},{3,2},{4,5},{5,4},{6,7},{7,6},{8,9},{9,8},{10,11... | collective-permute-start | bytes 1572872 | tf_op jit(solution)/shard_map/ppermute | solution.py:21
  20.9 74.5 %collective-permute-start.18 = (bf16[512,1024]{1,0:T(8,128)(2,1)S(1)}, bf16[512,1024]{1,0:T(8,128)(2,1)}, u32[]{:S(2)}, u32[]{:S(2)}) collective-permute-start(bf16[512,1024]{1,0:T(8,128)(2,1)S(1)} %copy-done), channel_id=1, source_target_pairs={{0,1},{1,0},{2,3},{3,2},{4,5},{5,4},{6,7},{7,6},{8,9},{9,8},{10,11... | collective-permute-start | bytes 3145736 | tf_op jit(solution)/shard_map/ppermute | solution.py:21
  21.5 59.9 %collective-permute-start.21 = (bf16[512,512]{1,0:T(8,128)(2,1)}, bf16[512,512]{1,0:T(8,128)(2,1)}, u32[]{:S(2)}, u32[]{:S(2)}) collective-permute-start(bf16[512,512]{1,0:T(8,128)(2,1)} %get-tuple-element.26), channel_id=1, source_target_pairs={{0,1},{1,0},{2,3},{3,2},{4,5},{5,4},{6,7},{7,6},{8,9},{9,8},{10,11... | collective-permute-start | bytes 1572872 | tf_op jit(solution)/shard_map/ppermute | solution.py:21
  24.9 11.5 %copy-start.18 = (s32[1,1,4,32]{3,2,1,0:T(4,128)S(1)}, s32[1,1,4,32]{3,2,1,0:T(4,128)}, u32[]{:S(2)}) copy-start(s32[1,1,4,32]{3,2,1,0:T(4,128)} %param.11) | copy-start | bytes 1540
  24.9 11.5 %copy-start.1 = (f32[1,512,1024]{2,1,0:T(8,128)S(1)}, f32[1,512,1024]{2,1,0:T(8,128)}, u32[]{:S(2)}) copy-start(f32[1,512,1024]{2,1,0:T(8,128)} %param.8) | copy-start | bytes 6291460
  32.3 38.7 %all-to-all-start.1 = ((bf16[8,128,128]{2,1,0:T(8,128)(2,1)}), bf16[8,128,128]{2,1,0:T(8,128)(2,1)}, u32[]{:S(2)}, u32[]{:S(2)}) async-start(bf16[8,128,128]{2,1,0:T(8,128)(2,1)} %slot_terms.1), calls=%async_computation.1 | async-start | bytes 524288 | tf_op jit(solution)/shard_map/all_to_all | solution.py:335
  40.6 36.0 %collective-permute-start = (s32[1,8,4,32]{3,0,2,1:T(1,128)S(1)}, s32[1,8,4,32]{3,0,2,1:T(1,128)S(1)}, u32[]{:S(2)}, u32[]{:S(2)}) collective-permute-start(s32[1,8,4,32]{3,0,2,1:T(1,128)S(1)} %bitcast.35), channel_id=1, source_target_pairs={{0,16},{8,24},{16,0},{24,8},{1,17},{9,25},{17,1},{25,9},{2,18},{10... | collective-permute-start | bytes 12296 | tf_op jit(solution)/shard_map/ppermute | solution.py:21
  43.0 38.9 %collective-permute-start.5 = (bf16[2,128,1024]{2,1,0:T(8,128)(2,1)S(1)}, bf16[2,128,1024]{2,1,0:T(8,128)(2,1)}, u32[]{:S(2)}, u32[]{:S(2)}) collective-permute-start(bf16[2,128,1024]{2,1,0:T(8,128)(2,1)S(1)} %pad_maximum_fusion.3), channel_id=1, source_target_pairs={{0,1},{1,0},{2,3},{3,2},{4,5},{5,4},{6,7},{7,6},{8,9},{9,8},{10,11... | collective-permute-start | bytes 1572872 | tf_op jit(solution)/shard_map/ppermute | solution.py:21
  72.9 12.8 %all-to-all-start.2 = ((bf16[8,4,32,128]{3,2,1,0:T(8,128)(2,1)}), bf16[8,4,32,128]{3,2,1,0:T(8,128)(2,1)S(1)}, u32[]{:S(2)}, u32[]{:S(2)}) async-start(bf16[8,4,32,128]{3,2,1,0:T(8,128)(2,1)} %broadcast_in_dim.53), calls=%async_computation.2 | async-start | bytes 524288 | tf_op jit(solution)/shard_map/all_to_all | solution.py:27
  76.6 1.3 collective-permute-start.1
  77.9 15.9 %collective-permute-start.6 = (bf16[2,128,1024]{2,1,0:T(8,128)(2,1)S(1)}, bf16[2,128,1024]{2,1,0:T(8,128)(2,1)}, u32[]{:S(2)}, u32[]{:S(2)}) collective-permute-start(bf16[2,128,1024]{2,1,0:T(8,128)(2,1)S(1)} %pad_maximum_fusion.3), channel_id=1, source_target_pairs={{0,2},{1,3},{2,0},{3,1},{4,6},{5,7},{6,4},{7,5},{8,10},{9,11},{10,... | collective-permute-start | bytes 1572872 | tf_op jit(solution)/shard_map/ppermute | solution.py:21
  79.9 28.1 %collective-permute-start.24 = (bf16[512,512]{1,0:T(8,128)(2,1)}, bf16[512,512]{1,0:T(8,128)(2,1)S(1)}, u32[]{:S(2)}, u32[]{:S(2)}) collective-permute-start(bf16[512,512]{1,0:T(8,128)(2,1)} %get-tuple-element.29), channel_id=1, source_target_pairs={{0,1},{1,0},{2,3},{3,2},{4,5},{5,4},{6,7},{7,6},{8,9},{9,8},{10,11... | collective-permute-start | bytes 1572872 | tf_op jit(solution)/shard_map/ppermute | solution.py:21
  81.4 27.2 %collective-permute-start.27 = (bf16[512,512]{1,0:T(8,128)(2,1)}, bf16[512,512]{1,0:T(8,128)(2,1)S(1)}, u32[]{:S(2)}, u32[]{:S(2)}) collective-permute-start(bf16[512,512]{1,0:T(8,128)(2,1)} %get-tuple-element.32), channel_id=1, source_target_pairs={{0,1},{1,0},{2,3},{3,2},{4,5},{5,4},{6,7},{7,6},{8,9},{9,8},{10,11... | collective-permute-start | bytes 1572872 | tf_op jit(solution)/shard_map/ppermute | solution.py:21
  85.7 23.3 %collective-permute-start.2 = (bf16[1,8,4,32,128]{4,3,2,1,0:T(8,128)(2,1)S(1)}, bf16[1,8,4,32,128]{4,3,2,1,0:T(8,128)(2,1)S(1)}, u32[]{:S(2)}, u32[]{:S(2)}) collective-permute-start(bf16[1,8,4,32,128]{4,3,2,1,0:T(8,128)(2,1)S(1)} %bitcast.30), channel_id=1, source_target_pairs={{0,16},{8,24},{16,0},{24,8},{1,17},{9,25},{17,1},{25,9},{2,18},{10... | collective-permute-start | bytes 786440 | tf_op jit(solution)/shard_map/ppermute | solution.py:21
  93.8 26.9 %collective-permute-start.7 = (bf16[2,128,1024]{2,1,0:T(8,128)(2,1)}, bf16[2,128,1024]{2,1,0:T(8,128)(2,1)}, u32[]{:S(2)}, u32[]{:S(2)}) collective-permute-start(bf16[2,128,1024]{2,1,0:T(8,128)(2,1)} %collective-permute-done.6), channel_id=1, source_target_pairs={{0,1},{1,0},{2,3},{3,2},{4,5},{5,4},{6,7},{7,6},{8,9},{9,8},{10,11... | collective-permute-start | bytes 1572872 | tf_op jit(solution)/shard_map/ppermute | solution.py:21
  95.4 25.8 %collective-permute-start.8 = (bf16[2,128,1024]{2,1,0:T(8,128)(2,1)}, bf16[2,128,1024]{2,1,0:T(8,128)(2,1)}, u32[]{:S(2)}, u32[]{:S(2)}) collective-permute-start(bf16[2,128,1024]{2,1,0:T(8,128)(2,1)} %collective-permute-done.5.refs_0_), channel_id=1, source_target_pairs={{0,16},{8,24},{16,0},{24,8},{1,17},{9,25},{17,1},{25,9},{2,18},{10... | collective-permute-start | bytes 1572872 | tf_op jit(solution)/shard_map/ppermute | solution.py:21
  98.2 36.7 %copy-start.2 = (bf16[4,128,1024]{2,1,0:T(8,128)(2,1)}, bf16[4,128,1024]{2,1,0:T(8,128)(2,1)S(1)}, u32[]{:S(2)}) copy-start(bf16[4,128,1024]{2,1,0:T(8,128)(2,1)S(1)} %pad_maximum_fusion.1.refs_0_) | copy-start | bytes 3145732
  108.0 2.6 %copy-start.12 = (bf16[512,512]{1,0:T(8,128)(2,1)}, bf16[512,512]{1,0:T(8,128)(2,1)S(1)}, u32[]{:S(2)}) copy-start(bf16[512,512]{1,0:T(8,128)(2,1)S(1)} %collective-permute-done.24.refs_4_) | copy-start | bytes 1572868
  108.0 52.9 %collective-permute-start.14 = (bf16[4,128,1024]{2,1,0:T(8,128)(2,1)S(1)}, bf16[4,128,1024]{2,1,0:T(8,128)(2,1)}, u32[]{:S(2)}, u32[]{:S(2)}) collective-permute-start(bf16[4,128,1024]{2,1,0:T(8,128)(2,1)S(1)} %pad_maximum_fusion.1.refs_0_), channel_id=1, source_target_pairs={{0,16},{8,24},{16,0},{24,8},{1,17},{9,25},{17,1},{25,9},{2,18},{10... | collective-permute-start | bytes 3145736 | tf_op jit(solution)/shard_map/ppermute | solution.py:21
  108.6 16.0 %collective-permute-start.19 = (bf16[2,128,1024]{2,1,0:T(8,128)(2,1)}, bf16[2,128,1024]{2,1,0:T(8,128)(2,1)}, u32[]{:S(2)}, u32[]{:S(2)}) collective-permute-start(bf16[2,128,1024]{2,1,0:T(8,128)(2,1)} %get-tuple-element.25), channel_id=1, source_target_pairs={{0,2},{1,3},{2,0},{3,1},{4,6},{5,7},{6,4},{7,5},{8,10},{9,11},{10,... | collective-permute-start | bytes 1572872 | tf_op jit(solution)/shard_map/ppermute | solution.py:21
  109.0 6.6 %copy-start.7 = (bf16[1,8,4,32,128]{4,3,2,1,0:T(8,128)(2,1)}, bf16[1,8,4,32,128]{4,3,2,1,0:T(8,128)(2,1)S(1)}, u32[]{:S(2)}) copy-start(bf16[1,8,4,32,128]{4,3,2,1,0:T(8,128)(2,1)S(1)} %collective-permute-done.2) | copy-start | bytes 786436
  109.0 25.9 %collective-permute-start.22 = (bf16[2,128,1024]{2,1,0:T(8,128)(2,1)}, bf16[2,128,1024]{2,1,0:T(8,128)(2,1)}, u32[]{:S(2)}, u32[]{:S(2)}) collective-permute-start(bf16[2,128,1024]{2,1,0:T(8,128)(2,1)} %get-tuple-element.28), channel_id=1, source_target_pairs={{0,2},{1,3},{2,0},{3,1},{4,6},{5,7},{6,4},{7,5},{8,10},{9,11},{10,... | collective-permute-start | bytes 1572872 | tf_op jit(solution)/shard_map/ppermute | solution.py:21
  115.6 19.4 %copy-start.3 = (f32[2,128,1024]{2,1,0:T(8,128)S(1)}, f32[2,128,1024]{2,1,0:T(8,128)}, u32[]{:S(2)}) copy-start(f32[2,128,1024]{2,1,0:T(8,128)} %get-tuple-element.24.refs_0_) | copy-start | bytes 3145732
  120.7 15.4 %copy-start.4 = (f32[2,128,1024]{2,1,0:T(8,128)S(1)}, f32[2,128,1024]{2,1,0:T(8,128)}, u32[]{:S(2)}) copy-start(f32[2,128,1024]{2,1,0:T(8,128)} %get-tuple-element.27.refs_0_) | copy-start | bytes 3145732
  120.7 28.3 %collective-permute-start.25 = (bf16[2,128,1024]{2,1,0:T(8,128)(2,1)}, bf16[2,128,1024]{2,1,0:T(8,128)(2,1)}, u32[]{:S(2)}, u32[]{:S(2)}) collective-permute-start(bf16[2,128,1024]{2,1,0:T(8,128)(2,1)} %get-tuple-element.31), channel_id=1, source_target_pairs={{0,2},{1,3},{2,0},{3,1},{4,6},{5,7},{6,4},{7,5},{8,10},{9,11},{10,... | collective-permute-start | bytes 1572872 | tf_op jit(solution)/shard_map/ppermute | solution.py:21
  121.2 39.7 %collective-permute-start.28 = (bf16[2,128,1024]{2,1,0:T(8,128)(2,1)}, bf16[2,128,1024]{2,1,0:T(8,128)(2,1)}, u32[]{:S(2)}, u32[]{:S(2)}) collective-permute-start(bf16[2,128,1024]{2,1,0:T(8,128)(2,1)} %get-tuple-element.34), channel_id=1, source_target_pairs={{0,2},{1,3},{2,0},{3,1},{4,6},{5,7},{6,4},{7,5},{8,10},{9,11},{10,... | collective-permute-start | bytes 1572872 | tf_op jit(solution)/shard_map/ppermute | solution.py:21
  124.6 36.3 %collective-permute-start.3 = (bf16[2,8,4,32,128]{4,3,2,1,0:T(8,128)(2,1)}, bf16[2,8,4,32,128]{4,3,2,1,0:T(8,128)(2,1)}, u32[]{:S(2)}, u32[]{:S(2)}) collective-permute-start(bf16[2,8,4,32,128]{4,3,2,1,0:T(8,128)(2,1)} %pad_maximum_fusion.2), channel_id=1, source_target_pairs={{0,8},{8,0},{16,24},{24,16},{1,9},{9,1},{17,25},{25,17},{2,10},{10... | collective-permute-start | bytes 1572872 | tf_op jit(solution)/shard_map/ppermute | solution.py:21
  134.9 61.0 %collective-permute-start.15 = (bf16[4,128,1024]{2,1,0:T(8,128)(2,1)S(1)}, bf16[4,128,1024]{2,1,0:T(8,128)(2,1)}, u32[]{:S(2)}, u32[]{:S(2)}) collective-permute-start(bf16[4,128,1024]{2,1,0:T(8,128)(2,1)S(1)} %pad_maximum_fusion.1.refs_0_), channel_id=1, source_target_pairs={{0,8},{8,0},{16,24},{24,16},{1,9},{9,1},{17,25},{25,17},{2,10},{10... | collective-permute-start | bytes 3145736 | tf_op jit(solution)/shard_map/ppermute | solution.py:21
  134.9 27.5 %copy-start.5 = (f32[2,128,1024]{2,1,0:T(8,128)S(1)}, f32[2,128,1024]{2,1,0:T(8,128)}, u32[]{:S(2)}) copy-start(f32[2,128,1024]{2,1,0:T(8,128)} %get-tuple-element.30.refs_3_) | copy-start | bytes 3145732
  134.9 28.6 %copy-start.6 = (f32[2,128,1024]{2,1,0:T(8,128)S(1)}, f32[2,128,1024]{2,1,0:T(8,128)}, u32[]{:S(2)}) copy-start(f32[2,128,1024]{2,1,0:T(8,128)} %get-tuple-element.33.refs_6_) | copy-start | bytes 3145732
  136.1 62.8 %copy-start.8 = (bf16[1,8,4,32,128]{4,3,2,1,0:T(8,128)(2,1)S(1)}, bf16[1,8,4,32,128]{4,3,2,1,0:T(8,128)(2,1)}, u32[]{:S(2)}) copy-start(bf16[1,8,4,32,128]{4,3,2,1,0:T(8,128)(2,1)} %copy-done.7) | copy-start | bytes 786436
  149.0 15.6 %collective-permute-start.20 = (bf16[1,128,1024]{2,1,0:T(8,128)(2,1)S(1)}, bf16[1,128,1024]{2,1,0:T(8,128)(2,1)S(1)}, u32[]{:S(2)}, u32[]{:S(2)}) collective-permute-start(bf16[1,128,1024]{2,1,0:T(8,128)(2,1)S(1)} %fusion.3), channel_id=1, source_target_pairs={{0,4},{1,5},{2,6},{3,7},{4,0},{5,1},{6,2},{7,3},{8,12},{9,13},{10,... | collective-permute-start | bytes 786440 | tf_op jit(solution)/shard_map/ppermute | solution.py:21
  160.9 17.7 %collective-permute-start.23 = (bf16[1,128,1024]{2,1,0:T(8,128)(2,1)S(1)}, bf16[1,128,1024]{2,1,0:T(8,128)(2,1)S(1)}, u32[]{:S(2)}, u32[]{:S(2)}) collective-permute-start(bf16[1,128,1024]{2,1,0:T(8,128)(2,1)S(1)} %fusion.2), channel_id=1, source_target_pairs={{0,4},{1,5},{2,6},{3,7},{4,0},{5,1},{6,2},{7,3},{8,12},{9,13},{10,... | collective-permute-start | bytes 786440 | tf_op jit(solution)/shard_map/ppermute | solution.py:21
  160.9 48.5 %collective-permute-start.16 = (bf16[4,128,1024]{2,1,0:T(8,128)(2,1)}, bf16[4,128,1024]{2,1,0:T(8,128)(2,1)S(1)}, u32[]{:S(2)}, u32[]{:S(2)}) collective-permute-start(bf16[4,128,1024]{2,1,0:T(8,128)(2,1)} %collective-permute-done.14.refs_1_), channel_id=1, source_target_pairs={{0,8},{8,0},{16,24},{24,16},{1,9},{9,1},{17,25},{25,17},{2,10},{10... | collective-permute-start | bytes 3145736 | tf_op jit(solution)/shard_map/ppermute | solution.py:21
  160.9 34.6 %collective-permute-start.9 = (bf16[2,128,1024]{2,1,0:T(8,128)(2,1)}, bf16[2,128,1024]{2,1,0:T(8,128)(2,1)S(1)}, u32[]{:S(2)}, u32[]{:S(2)}) collective-permute-start(bf16[2,128,1024]{2,1,0:T(8,128)(2,1)} %collective-permute-done.7.refs_1_), channel_id=1, source_target_pairs={{0,16},{8,24},{16,0},{24,8},{1,17},{9,25},{17,1},{25,9},{2,18},{10... | collective-permute-start | bytes 1572872 | tf_op jit(solution)/shard_map/ppermute | solution.py:21
  164.5 41.8 %copy-start.14 = (bf16[1,128,1024]{2,1,0:T(8,128)(2,1)}, bf16[1,128,1024]{2,1,0:T(8,128)(2,1)S(1)}, u32[]{:S(2)}) copy-start(bf16[1,128,1024]{2,1,0:T(8,128)(2,1)S(1)} %collective-permute-done.20.refs_2_) | copy-start | bytes 786436
  164.6 25.2 %collective-permute-start.26 = (bf16[1,128,1024]{2,1,0:T(8,128)(2,1)S(1)}, bf16[1,128,1024]{2,1,0:T(8,128)(2,1)S(1)}, u32[]{:S(2)}, u32[]{:S(2)}) collective-permute-start(bf16[1,128,1024]{2,1,0:T(8,128)(2,1)S(1)} %fusion.1), channel_id=1, source_target_pairs={{0,4},{1,5},{2,6},{3,7},{4,0},{5,1},{6,2},{7,3},{8,12},{9,13},{10,... | collective-permute-start | bytes 786440 | tf_op jit(solution)/shard_map/ppermute | solution.py:21
  178.6 17.3 %copy-start.15 = (bf16[1,128,1024]{2,1,0:T(8,128)(2,1)}, bf16[1,128,1024]{2,1,0:T(8,128)(2,1)S(1)}, u32[]{:S(2)}) copy-start(bf16[1,128,1024]{2,1,0:T(8,128)(2,1)S(1)} %collective-permute-done.23.refs_2_) | copy-start | bytes 786436
  178.6 16.8 %collective-permute-start.29 = (bf16[1,128,1024]{2,1,0:T(8,128)(2,1)S(1)}, bf16[1,128,1024]{2,1,0:T(8,128)(2,1)S(1)}, u32[]{:S(2)}, u32[]{:S(2)}) collective-permute-start(bf16[1,128,1024]{2,1,0:T(8,128)(2,1)S(1)} %fusion), channel_id=1, source_target_pairs={{0,4},{1,5},{2,6},{3,7},{4,0},{5,1},{6,2},{7,3},{8,12},{9,13},{10,... | collective-permute-start | bytes 786440 | tf_op jit(solution)/shard_map/ppermute | solution.py:21
  189.8 6.1 %copy-start.16 = (bf16[1,128,1024]{2,1,0:T(8,128)(2,1)}, bf16[1,128,1024]{2,1,0:T(8,128)(2,1)S(1)}, u32[]{:S(2)}) copy-start(bf16[1,128,1024]{2,1,0:T(8,128)(2,1)S(1)} %collective-permute-done.26.refs_5_) | copy-start | bytes 786436
  189.8 28.9 %collective-permute-start.10 = (bf16[2,128,1024]{2,1,0:T(8,128)(2,1)}, bf16[2,128,1024]{2,1,0:T(8,128)(2,1)}, u32[]{:S(2)}, u32[]{:S(2)}) collective-permute-start(bf16[2,128,1024]{2,1,0:T(8,128)(2,1)} %collective-permute-done.5.refs_0_), channel_id=1, source_target_pairs={{0,8},{8,0},{16,24},{24,16},{1,9},{9,1},{17,25},{25,17},{2,10},{10... | collective-permute-start | bytes 1572872 | tf_op jit(solution)/shard_map/ppermute | solution.py:21
  195.4 23.4 %collective-permute-start.11 = (bf16[2,128,1024]{2,1,0:T(8,128)(2,1)}, bf16[2,128,1024]{2,1,0:T(8,128)(2,1)}, u32[]{:S(2)}, u32[]{:S(2)}) collective-permute-start(bf16[2,128,1024]{2,1,0:T(8,128)(2,1)} %collective-permute-done.7.refs_1_), channel_id=1, source_target_pairs={{0,8},{8,0},{16,24},{24,16},{1,9},{9,1},{17,25},{25,17},{2,10},{10... | collective-permute-start | bytes 1572872 | tf_op jit(solution)/shard_map/ppermute | solution.py:21
  195.5 10.9 %copy-start.10 = (bf16[2,128,1024]{2,1,0:T(8,128)(2,1)}, bf16[2,128,1024]{2,1,0:T(8,128)(2,1)S(1)}, u32[]{:S(2)}) copy-start(bf16[2,128,1024]{2,1,0:T(8,128)(2,1)S(1)} %collective-permute-done.9.refs_3_) | copy-start | bytes 1572868
  195.5 23.3 %collective-permute-start.12 = (bf16[2,128,1024]{2,1,0:T(8,128)(2,1)}, bf16[2,128,1024]{2,1,0:T(8,128)(2,1)}, u32[]{:S(2)}, u32[]{:S(2)}) collective-permute-start(bf16[2,128,1024]{2,1,0:T(8,128)(2,1)} %collective-permute-done.8.refs_2_), channel_id=1, source_target_pairs={{0,8},{8,0},{16,24},{24,16},{1,9},{9,1},{17,25},{25,17},{2,10},{10... | collective-permute-start | bytes 1572872 | tf_op jit(solution)/shard_map/ppermute | solution.py:21
  196.1 22.7 %collective-permute-start.13 = (bf16[2,128,1024]{2,1,0:T(8,128)(2,1)S(1)}, bf16[2,128,1024]{2,1,0:T(8,128)(2,1)S(1)}, u32[]{:S(2)}, u32[]{:S(2)}) collective-permute-start(bf16[2,128,1024]{2,1,0:T(8,128)(2,1)S(1)} %collective-permute-done.9.refs_3_), channel_id=1, source_target_pairs={{0,8},{8,0},{16,24},{24,16},{1,9},{9,1},{17,25},{25,17},{2,10},{10... | collective-permute-start | bytes 1572872 | tf_op jit(solution)/shard_map/ppermute | solution.py:21
  (4 other events, 4.6 us)

commit v3 on v2

--- a/solution.py
+++ b/solution.py
@@ -396,9 +396,9 @@
         parts.append(terms)
     flat_index = index.reshape(1, islands * cap)
     new_error = None
-    for first, some in ((0, parts[:-1]), (chunks - 1, parts[-1:])):
-        if some:
-            new_error = error_step(place, some, first, flat_index, error[0], own_rows, scale, new_error)
+    cuts = sorted({0, min(1, chunks - 1), chunks - 1, chunks})
+    for first, end in zip(cuts, cuts[1:]):
+        new_error = error_step(place, parts[first:end], first, flat_index, error[0], own_rows, scale, new_error)
     new_error = new_error[None]
     return (new_weight, new_momentum, new_error)
 

time: 228 us -> 229 us (level)
    pallas_call x2 -> x3, Pallas kernels: 8.36 us -> 9.9 us  [error_step(): pl.pallas_call(body, grid_spec=pltpu.PrefetchScalarGridSpec(num_scalar_pr...]
  transfers between devices with their start and end apart: 33 -> 33, of which waited for: 10 -> 10; matrix products, arithmetic and copies ran while one was open for 10% -> 10% of each run, Pallas kernels for 21% -> 22%
where the time goes in v3:
time: 229 us; the launch traced here: 228 us
  waiting for transfers between devices  99.1 us (43%)
  Pallas kernels  57.2 us (25%)
  starting transfers between devices  43.7 us (19%)
  other arithmetic  14.9 us (7%)
  local copies, waits for them, and re-layouts  12.3 us (5%)
    ppermute x30, waiting for transfers between devices, swap(): return lax.ppermute(values, axis, [(i, i ^ 1 << bit) for i in range(size)])  69.4 us
    ppermute x30, starting transfers between devices, swap(): return lax.ppermute(values, axis, [(i, i ^ 1 << bit) for i in range(size)])  28.8 us
    all_to_all x1, waiting for transfers between devices, local(): lax.all_to_all(terms, 'inside', split_axis=0, concat_axis=0, tiled=True)  26 us
    pallas_call x4, Pallas kernels, pair_dot(): pl.pallas_call(body, grid_spec=pltpu.PrefetchScalarGridSpec(num_scalar_pr...  19.8 us
    pallas_call x2, Pallas kernels, weight_step(): pl.pallas_call(body, grid_spec=pltpu.PrefetchScalarGridSpec(num_scalar_pr...  15.4 us
    all_to_all x2, starting transfers between devices, spread(): lax.all_to_all(every, 'inside', split_axis=0, concat_axis=0, tiled=True)  10.9 us
    pallas_call x3, Pallas kernels, error_step(): pl.pallas_call(body, grid_spec=pltpu.PrefetchScalarGridSpec(num_scalar_pr...  9.9 us
    pallas_call x1, Pallas kernels, slot_terms(): pl.pallas_call(body, grid_spec=pltpu.PrefetchScalarGridSpec(num_scalar_pr...  7.44 us
  transfers between devices with their start and end apart: 33, of which 10 were waited for; matrix products, arithmetic and copies ran while one was open for 10% of the time, Pallas kernels for 22%

profile of v3, /device:TPU:0, one launch (start us, length us, event | category | flops | bytes accessed | tf_op | source)
XLA Modules:
  0.0 228.2 jit_solution(6445793868041812522)
XLA Ops:
  2.0 7.3 %all-to-all-start = ((s32[8,1,128]{2,1,0:T(1,128)}), s32[8,1,128]{2,1,0:T(1,128)S(1)}, u32[]{:S(2)}, u32[]{:S(2)}) async-start(s32[8,1,128]{2,1,0:T(1,128)} %reshape.93), calls=%async_computation | async-start | bytes 8192 | tf_op jit(solution)/shard_map/all_to_all | solution.py:27
  9.3 1.9 fusion.4
  11.2 2.9 %collective-permute-start.4 = (bf16[1,128,1024]{2,1,0:T(8,128)(2,1)}, bf16[1,128,1024]{2,1,0:T(8,128)(2,1)}, u32[]{:S(2)}, u32[]{:S(2)}) collective-permute-start(bf16[1,128,1024]{2,1,0:T(8,128)(2,1)} %fusion.4), channel_id=1, source_target_pairs={{0,4},{1,5},{2,6},{3,7},{4,0},{5,1},{6,2},{7,3},{8,12},{9,13},{10,... | collective-permute-start | bytes 786440 | tf_op jit(solution)/shard_map/ppermute | solution.py:21
  14.7 4.7 %take_halves.1 = (bf16[512,512]{1,0:T(8,128)(2,1)}, bf16[512,512]{1,0:T(8,128)(2,1)}, bf16[512,512]{1,0:T(8,128)(2,1)}, bf16[512,512]{1,0:T(8,128)(2,1)}) custom-call(s32[3]{0:T(128)} %pad_add_fusion.1.p, bf16[512,4096]{1,0:T(8,128)(2,1)} %refs_3_.7), custom_call_target="tpu_custom_call" | custom-call | tf_op jit(solution)/shard_map/take_halves/pallas_call | solution.py:48
  19.4 1.5 collective-permute-start.17
  21.5 1.5 collective-permute-start.21
  24.9 7.4 %slot_terms.1 = bf16[8,128,128]{2,1,0:T(8,128)(2,1)} custom-call(s32[3]{0:T(128)} %pad_add_fusion.1.p, s32[8,1,128]{2,1,0:T(1,128)} %reshape.79.ix, bf16[512,4096]{1,0:T(8,128)(2,1)} %refs_3_.7, bf16[512,1024]{1,0:T(8,128)(2,1)} %refs_5_.7), custom_call_target="tpu_custom_call" | custom-call | tf_op jit(solution)/shard_map/slot_terms/pallas_call | solution.py:143
  32.3 4.1 %all-to-all-start.1 = ((bf16[8,128,128]{2,1,0:T(8,128)(2,1)}), bf16[8,128,128]{2,1,0:T(8,128)(2,1)}, u32[]{:S(2)}, u32[]{:S(2)}) async-start(bf16[8,128,128]{2,1,0:T(8,128)(2,1)} %slot_terms.1), calls=%async_computation.1 | async-start | bytes 524288 | tf_op jit(solution)/shard_map/all_to_all | solution.py:335
  36.4 1.5 reshape_squeeze.6
  38.0 2.6 %gather_fusion = f32[128,128]{1,0:T(8,128)S(1)} fusion(f32[4,1024,128]{2,1,0:T(8,128)} %reshape_squeeze.6, s32[128]{0:T(128)S(1)} %reshape.82), kind=kCustom, calls=%fused_computation | custom fusion | bytes 132096 | tf_op jit(solution)/shard_map/jit(take_along_axis)/gather | solution.py:361
  40.6 1.4 collective-permute-start
  41.9 1.1 pad_maximum_fusion.3
  43.0 2.0 collective-permute-start.5
  45.1 26.0 %all-to-all-done.1 = bf16[8,128,128]{2,1,0:T(8,128)(2,1)} async-done(((bf16[8,128,128]{2,1,0:T(8,128)(2,1)}), bf16[8,128,128]{2,1,0:T(8,128)(2,1)}, u32[]{:S(2)}, u32[]{:S(2)}) %all-to-all-start.1) | async-done | bytes 262176 | tf_op jit(solution)/shard_map/all_to_all | solution.py:335
  72.9 3.6 %all-to-all-start.2 = ((bf16[8,4,32,128]{3,2,1,0:T(8,128)(2,1)}), bf16[8,4,32,128]{3,2,1,0:T(8,128)(2,1)S(1)}, u32[]{:S(2)}, u32[]{:S(2)}) async-start(bf16[8,4,32,128]{3,2,1,0:T(8,128)(2,1)} %broadcast_in_dim.53), calls=%async_computation.2 | async-start | bytes 524288 | tf_op jit(solution)/shard_map/all_to_all | solution.py:27
  76.7 1.2 collective-permute-done.1
  77.9 2.0 collective-permute-start.6
  79.9 1.5 collective-permute-start.24
  81.9 3.7 %all-to-all-done.2 = bf16[8,4,32,128]{3,2,1,0:T(8,128)(2,1)S(1)} async-done(((bf16[8,4,32,128]{3,2,1,0:T(8,128)(2,1)}), bf16[8,4,32,128]{3,2,1,0:T(8,128)(2,1)S(1)}, u32[]{:S(2)}, u32[]{:S(2)}) %all-to-all-start.2) | async-done | bytes 262176 | tf_op jit(solution)/shard_map/all_to_all | solution.py:27
  85.7 1.5 collective-permute-start.2
  87.2 6.6 %collective-permute-done.6 = bf16[2,128,1024]{2,1,0:T(8,128)(2,1)} collective-permute-done((bf16[2,128,1024]{2,1,0:T(8,128)(2,1)S(1)}, bf16[2,128,1024]{2,1,0:T(8,128)(2,1)}, u32[]{:S(2)}, u32[]{:S(2)}) %collective-permute-start.6) | collective-permute-done | bytes 524320 | tf_op jit(solution)/shard_map/ppermute | solution.py:21
  93.8 1.6 collective-permute-start.7
  95.4 1.5 collective-permute-start.8
  96.9 1.3 pad_maximum_fusion.1.refs_0_
  98.2 4.9 %pair_dot.4 = (bf16[2,128,1024]{2,1,0:T(8,128)(2,1)}, f32[2,128,1024]{2,1,0:T(8,128)}) custom-call(s32[3]{0:T(128)} %pad_add_fusion.1.p, bf16[512,4096]{1,0:T(8,128)(2,1)} %refs_3_.7, bf16[512,4096]{1,0:T(8,128)(2,1)} %refs_3_.7, bf16[512,4096]{1,0:T(8,128)(2,1)} %refs_3_.7, bf16[512,4096]{1,0:T(8,128)(2,1)} %refs_3_.7, ...), custom_call_target="tpu_custom_call" | custom-call | tf_op jit(solution)/shard_map/pair_dot/pallas_call | solution.py:95
  103.1 4.9 %pair_dot.5 = (bf16[2,128,1024]{2,1,0:T(8,128)(2,1)}, f32[2,128,1024]{2,1,0:T(8,128)}) custom-call(s32[3]{0:T(128)} %pad_add_fusion.1.p, bf16[512,4096]{1,0:T(8,128)(2,1)} %refs_3_.7, bf16[512,4096]{1,0:T(8,128)(2,1)} %refs_3_.7, bf16[512,4096]{1,0:T(8,128)(2,1)} %refs_3_.7, bf16[512,4096]{1,0:T(8,128)(2,1)} %refs_3_.7, ...), custom_call_target="tpu_custom_call" | custom-call | tf_op jit(solution)/shard_map/pair_dot/pallas_call | solution.py:95
  109.0 1.6 collective-permute-start.22
  110.6 4.9 %pair_dot.6 = (bf16[2,128,1024]{2,1,0:T(8,128)(2,1)}, f32[2,128,1024]{2,1,0:T(8,128)}) custom-call(s32[3]{0:T(128)} %pad_add_fusion.1.p, bf16[512,4096]{1,0:T(8,128)(2,1)} %refs_3_.7, bf16[512,4096]{1,0:T(8,128)(2,1)} %refs_3_.7, bf16[512,4096]{1,0:T(8,128)(2,1)} %refs_3_.7, bf16[512,4096]{1,0:T(8,128)(2,1)} %refs_3_.7, bf16[512,512]{1,0:T(8,128)(2,1)} %copy-done.12, ...), custom_call_target="tpu_custom_call" | custom-call | tf_op jit(solution)/shard_map/pair_dot/pallas_call | solution.py:95
  115.6 5.1 %pair_dot.7 = (bf16[2,128,1024]{2,1,0:T(8,128)(2,1)}, f32[2,128,1024]{2,1,0:T(8,128)}) custom-call(s32[3]{0:T(128)} %pad_add_fusion.1.p, bf16[512,4096]{1,0:T(8,128)(2,1)} %refs_3_.7, bf16[512,4096]{1,0:T(8,128)(2,1)} %refs_3_.7, bf16[512,4096]{1,0:T(8,128)(2,1)} %refs_3_.7, bf16[512,4096]{1,0:T(8,128)(2,1)} %refs_3_.7, bf16[512,512]{1,0:T(8,128)(2,1)} %copy-done.13, ...), custom_call_target="tpu_custom_call" | custom-call | tf_op jit(solution)/shard_map/pair_dot/pallas_call | solution.py:95
  121.1 1.6 collective-permute-start.28
  122.8 1.8 pad_maximum_fusion.2
  124.6 10.4 %collective-permute-done.22.refs_1_ = bf16[2,128,1024]{2,1,0:T(8,128)(2,1)} collective-permute-done((bf16[2,128,1024]{2,1,0:T(8,128)(2,1)}, bf16[2,128,1024]{2,1,0:T(8,128)(2,1)}, u32[]{:S(2)}, u32[]{:S(2)}) %collective-permute-start.22) | collective-permute-done | bytes 524320 | tf_op jit(solution)/shard_map/ppermute | solution.py:21
  135.0 1.2 fusion.3
  136.1 1.0 fusion.2
  137.2 11.8 %collective-permute-done.25.refs_4_ = bf16[2,128,1024]{2,1,0:T(8,128)(2,1)} collective-permute-done((bf16[2,128,1024]{2,1,0:T(8,128)(2,1)}, bf16[2,128,1024]{2,1,0:T(8,128)(2,1)}, u32[]{:S(2)}, u32[]{:S(2)}) %collective-permute-start.25) | collective-permute-done | bytes 524320 | tf_op jit(solution)/shard_map/ppermute | solution.py:21
  149.3 11.6 %collective-permute-done.28.refs_1_ = bf16[2,128,1024]{2,1,0:T(8,128)(2,1)} collective-permute-done((bf16[2,128,1024]{2,1,0:T(8,128)(2,1)}, bf16[2,128,1024]{2,1,0:T(8,128)(2,1)}, u32[]{:S(2)}, u32[]{:S(2)}) %collective-permute-start.28) | collective-permute-done | bytes 524320 | tf_op jit(solution)/shard_map/ppermute | solution.py:21
  160.9 1.6 collective-permute-start.9
  163.5 1.0 fusion
  164.6 3.0 %collective-permute-start.26 = (bf16[1,128,1024]{2,1,0:T(8,128)(2,1)S(1)}, bf16[1,128,1024]{2,1,0:T(8,128)(2,1)S(1)}, u32[]{:S(2)}, u32[]{:S(2)}) collective-permute-start(bf16[1,128,1024]{2,1,0:T(8,128)(2,1)S(1)} %fusion.1), channel_id=1, source_target_pairs={{0,4},{1,5},{2,6},{3,7},{4,0},{5,1},{6,2},{7,3},{8,12},{9,13},{10,... | collective-permute-start | bytes 786440 | tf_op jit(solution)/shard_map/ppermute | solution.py:21
  167.5 11.0 %collective-permute-done.23.refs_2_ = bf16[1,128,1024]{2,1,0:T(8,128)(2,1)S(1)} collective-permute-done((bf16[1,128,1024]{2,1,0:T(8,128)(2,1)S(1)}, bf16[1,128,1024]{2,1,0:T(8,128)(2,1)S(1)}, u32[]{:S(2)}, u32[]{:S(2)}) %collective-permute-start.23) | collective-permute-done | bytes 262176 | tf_op jit(solution)/shard_map/ppermute | solution.py:21
  178.6 11.2 %collective-permute-done.26.refs_5_ = bf16[1,128,1024]{2,1,0:T(8,128)(2,1)S(1)} collective-permute-done((bf16[1,128,1024]{2,1,0:T(8,128)(2,1)S(1)}, bf16[1,128,1024]{2,1,0:T(8,128)(2,1)S(1)}, u32[]{:S(2)}, u32[]{:S(2)}) %collective-permute-start.26) | collective-permute-done | bytes 262176 | tf_op jit(solution)/shard_map/ppermute | solution.py:21
  189.8 5.5 %collective-permute-done.29.refs_2_ = bf16[1,128,1024]{2,1,0:T(8,128)(2,1)S(1)} collective-permute-done((bf16[1,128,1024]{2,1,0:T(8,128)(2,1)S(1)}, bf16[1,128,1024]{2,1,0:T(8,128)(2,1)S(1)}, u32[]{:S(2)}, u32[]{:S(2)}) %collective-permute-start.29) | collective-permute-done | bytes 262176 | tf_op jit(solution)/shard_map/ppermute | solution.py:21
  198.9 2.1 pad_maximum_fusion.v
  201.0 3.1 %error_step.3.refs_6_ = f32[512,1024]{1,0:T(8,128)} custom-call(s32[3]{0:T(128)} %pad_add_fusion.1.p, s32[1,128]{1,0:T(1,128)} %reshape_squeeze.7.ix, f32[512,1024]{1,0:T(8,128)} %bitcast.26, f32[2,128,1024]{2,1,0:T(8,128)} %get-tuple-element.33.refs_0_, bf16[2,128,1024]{2,1,0:T(8,128)(2,1)} %collective-permute-done.28.refs_1_, bf16[1,128,1024]{2,1,0:T(8,128)(2,1)} %copy-done.17), custom_call_target="tpu_custom_call" | custom-call | tf_op jit(solution)/shard_map/error_step/pallas_call | solution.py:217
  204.1 3.8 %error_step.4.refs_3_ = f32[512,1024]{1,0:T(8,128)} custom-call(s32[3]{0:T(128)} %pad_add_fusion.1.p, s32[1,128]{1,0:T(1,128)} %reshape_squeeze.7.ix, f32[512,1024]{1,0:T(8,128)} %bitcast.27, f32[2,128,1024]{2,1,0:T(8,128)} %get-tuple-element.27.refs_0_, bf16[2,128,1024]{2,1,0:T(8,128)(2,1)} %collective-permute-done.22.refs_1_, ...), custom_call_target="tpu_custom_call", output_to_operand_aliasing={{}: (9, {})} | custom-call | tf_op jit(solution)/shard_map/error_step/pallas_call | solution.py:217
  207.9 3.1 %error_step.5 = f32[512,1024]{1,0:T(8,128)} custom-call(s32[3]{0:T(128)} %pad_add_fusion.1.p, s32[1,128]{1,0:T(1,128)} %reshape_squeeze.7.ix, f32[512,1024]{1,0:T(8,128)} %bitcast.28, f32[2,128,1024]{2,1,0:T(8,128)} %get-tuple-element.24.refs_0_, bf16[2,128,1024]{2,1,0:T(8,128)(2,1)} %collective-permute-done.19.refs_1_, ...), custom_call_target="tpu_custom_call", output_to_operand_aliasing={{}: (6, {})} | custom-call | tf_op jit(solution)/shard_map/error_step/pallas_call | solution.py:217
  211.9 8.3 %weight_step.2 = (bf16[4,2,4,128,1024]{4,3,2,1,0:T(8,128)(2,1)}, f32[512,1024]{1,0:T(8,128)}) custom-call(s32[6]{0:T(128)} %stack.50.w, s32[8,4,1,128]{3,2,1,0:T(1,128)} %reshape.80.ix, bf16[4,8,4,32,128]{4,3,2,1,0:T(8,128)(2,1)} %pad_maximum_fusion.v, bf16[4,128,1024]{2,1,0:T(8,128)(2,1)} %copy-done.2, ...), custom_call_target="tpu_custom_call" | custom-call | tf_op jit(solution)/shard_map/weight_step/pallas_call | solution.py:283
  221.2 7.0 %weight_step.3 = bf16[4,2,4,128,1024]{4,3,2,1,0:T(8,128)(2,1)} custom-call(s32[6]{0:T(128)} %stack.46.w, s32[8,4,1,128]{3,2,1,0:T(1,128)} %reshape.80.ix, bf16[4,8,4,32,128]{4,3,2,1,0:T(8,128)(2,1)} %pad_maximum_fusion.v, bf16[2,128,1024]{2,1,0:T(8,128)(2,1)} %collective-permute-done.5.refs_0_, ...), custom_call_target="tpu_custom_call", output_to_operand_aliasing={{}: (11, {})} | custom-call | tf_op jit(solution)/shard_map/weight_step/pallas_call | solution.py:283
  (98 shorter events, 15.4 us)
Async XLA Ops:
  2.0 20.9 %all-to-all-start = ((s32[8,1,128]{2,1,0:T(1,128)}), s32[8,1,128]{2,1,0:T(1,128)S(1)}, u32[]{:S(2)}, u32[]{:S(2)}) async-start(s32[8,1,128]{2,1,0:T(1,128)} %reshape.93), calls=%async_computation | async-start | bytes 8192 | tf_op jit(solution)/shard_map/all_to_all | solution.py:27
  11.2 30.8 %collective-permute-start.4 = (bf16[1,128,1024]{2,1,0:T(8,128)(2,1)}, bf16[1,128,1024]{2,1,0:T(8,128)(2,1)}, u32[]{:S(2)}, u32[]{:S(2)}) collective-permute-start(bf16[1,128,1024]{2,1,0:T(8,128)(2,1)} %fusion.4), channel_id=1, source_target_pairs={{0,4},{1,5},{2,6},{3,7},{4,0},{5,1},{6,2},{7,3},{8,12},{9,13},{10,... | collective-permute-start | bytes 786440 | tf_op jit(solution)/shard_map/ppermute | solution.py:21
  14.7 6.1 %copy-start.1 = (bf16[512,1024]{1,0:T(8,128)(2,1)S(1)}, bf16[512,1024]{1,0:T(8,128)(2,1)}, u32[]{:S(2)}) copy-start(bf16[512,1024]{1,0:T(8,128)(2,1)} %refs_5_.7) | copy-start | bytes 3145732
  19.4 60.5 %collective-permute-start.17 = (bf16[512,512]{1,0:T(8,128)(2,1)}, bf16[512,512]{1,0:T(8,128)(2,1)}, u32[]{:S(2)}, u32[]{:S(2)}) collective-permute-start(bf16[512,512]{1,0:T(8,128)(2,1)} %get-tuple-element.23), channel_id=1, source_target_pairs={{0,1},{1,0},{2,3},{3,2},{4,5},{5,4},{6,7},{7,6},{8,9},{9,8},{10,11... | collective-permute-start | bytes 1572872 | tf_op jit(solution)/shard_map/ppermute | solution.py:21
  20.9 74.5 %collective-permute-start.18 = (bf16[512,1024]{1,0:T(8,128)(2,1)S(1)}, bf16[512,1024]{1,0:T(8,128)(2,1)}, u32[]{:S(2)}, u32[]{:S(2)}) collective-permute-start(bf16[512,1024]{1,0:T(8,128)(2,1)S(1)} %copy-done.1), channel_id=1, source_target_pairs={{0,1},{1,0},{2,3},{3,2},{4,5},{5,4},{6,7},{7,6},{8,9},{9,8},{10,11... | collective-permute-start | bytes 3145736 | tf_op jit(solution)/shard_map/ppermute | solution.py:21
  21.5 59.9 %collective-permute-start.21 = (bf16[512,512]{1,0:T(8,128)(2,1)}, bf16[512,512]{1,0:T(8,128)(2,1)}, u32[]{:S(2)}, u32[]{:S(2)}) collective-permute-start(bf16[512,512]{1,0:T(8,128)(2,1)} %get-tuple-element.26), channel_id=1, source_target_pairs={{0,1},{1,0},{2,3},{3,2},{4,5},{5,4},{6,7},{7,6},{8,9},{9,8},{10,11... | collective-permute-start | bytes 1572872 | tf_op jit(solution)/shard_map/ppermute | solution.py:21
  24.9 11.5 %copy-start.18 = (s32[1,1,4,32]{3,2,1,0:T(4,128)S(1)}, s32[1,1,4,32]{3,2,1,0:T(4,128)}, u32[]{:S(2)}) copy-start(s32[1,1,4,32]{3,2,1,0:T(4,128)} %param.11) | copy-start | bytes 1540
  24.9 11.5 %copy-start = (f32[1,512,1024]{2,1,0:T(8,128)S(1)}, f32[1,512,1024]{2,1,0:T(8,128)}, u32[]{:S(2)}) copy-start(f32[1,512,1024]{2,1,0:T(8,128)} %param.8) | copy-start | bytes 6291460
  32.3 38.7 %all-to-all-start.1 = ((bf16[8,128,128]{2,1,0:T(8,128)(2,1)}), bf16[8,128,128]{2,1,0:T(8,128)(2,1)}, u32[]{:S(2)}, u32[]{:S(2)}) async-start(bf16[8,128,128]{2,1,0:T(8,128)(2,1)} %slot_terms.1), calls=%async_computation.1 | async-start | bytes 524288 | tf_op jit(solution)/shard_map/all_to_all | solution.py:335
  40.6 36.0 %collective-permute-start = (s32[1,8,4,32]{3,0,2,1:T(1,128)S(1)}, s32[1,8,4,32]{3,0,2,1:T(1,128)S(1)}, u32[]{:S(2)}, u32[]{:S(2)}) collective-permute-start(s32[1,8,4,32]{3,0,2,1:T(1,128)S(1)} %bitcast.36), channel_id=1, source_target_pairs={{0,16},{8,24},{16,0},{24,8},{1,17},{9,25},{17,1},{25,9},{2,18},{10... | collective-permute-start | bytes 12296 | tf_op jit(solution)/shard_map/ppermute | solution.py:21
  43.0 38.9 %collective-permute-start.5 = (bf16[2,128,1024]{2,1,0:T(8,128)(2,1)S(1)}, bf16[2,128,1024]{2,1,0:T(8,128)(2,1)}, u32[]{:S(2)}, u32[]{:S(2)}) collective-permute-start(bf16[2,128,1024]{2,1,0:T(8,128)(2,1)S(1)} %pad_maximum_fusion.3), channel_id=1, source_target_pairs={{0,1},{1,0},{2,3},{3,2},{4,5},{5,4},{6,7},{7,6},{8,9},{9,8},{10,11... | collective-permute-start | bytes 1572872 | tf_op jit(solution)/shard_map/ppermute | solution.py:21
  72.9 12.8 %all-to-all-start.2 = ((bf16[8,4,32,128]{3,2,1,0:T(8,128)(2,1)}), bf16[8,4,32,128]{3,2,1,0:T(8,128)(2,1)S(1)}, u32[]{:S(2)}, u32[]{:S(2)}) async-start(bf16[8,4,32,128]{3,2,1,0:T(8,128)(2,1)} %broadcast_in_dim.53), calls=%async_computation.2 | async-start | bytes 524288 | tf_op jit(solution)/shard_map/all_to_all | solution.py:27
  76.6 1.3 collective-permute-start.1
  77.9 15.9 %collective-permute-start.6 = (bf16[2,128,1024]{2,1,0:T(8,128)(2,1)S(1)}, bf16[2,128,1024]{2,1,0:T(8,128)(2,1)}, u32[]{:S(2)}, u32[]{:S(2)}) collective-permute-start(bf16[2,128,1024]{2,1,0:T(8,128)(2,1)S(1)} %pad_maximum_fusion.3), channel_id=1, source_target_pairs={{0,2},{1,3},{2,0},{3,1},{4,6},{5,7},{6,4},{7,5},{8,10},{9,11},{10,... | collective-permute-start | bytes 1572872 | tf_op jit(solution)/shard_map/ppermute | solution.py:21
  79.9 28.1 %collective-permute-start.24 = (bf16[512,512]{1,0:T(8,128)(2,1)}, bf16[512,512]{1,0:T(8,128)(2,1)S(1)}, u32[]{:S(2)}, u32[]{:S(2)}) collective-permute-start(bf16[512,512]{1,0:T(8,128)(2,1)} %get-tuple-element.29), channel_id=1, source_target_pairs={{0,1},{1,0},{2,3},{3,2},{4,5},{5,4},{6,7},{7,6},{8,9},{9,8},{10,11... | collective-permute-start | bytes 1572872 | tf_op jit(solution)/shard_map/ppermute | solution.py:21
  81.4 27.2 %collective-permute-start.27 = (bf16[512,512]{1,0:T(8,128)(2,1)}, bf16[512,512]{1,0:T(8,128)(2,1)S(1)}, u32[]{:S(2)}, u32[]{:S(2)}) collective-permute-start(bf16[512,512]{1,0:T(8,128)(2,1)} %get-tuple-element.32), channel_id=1, source_target_pairs={{0,1},{1,0},{2,3},{3,2},{4,5},{5,4},{6,7},{7,6},{8,9},{9,8},{10,11... | collective-permute-start | bytes 1572872 | tf_op jit(solution)/shard_map/ppermute | solution.py:21
  85.7 23.3 %collective-permute-start.2 = (bf16[1,8,4,32,128]{4,3,2,1,0:T(8,128)(2,1)S(1)}, bf16[1,8,4,32,128]{4,3,2,1,0:T(8,128)(2,1)S(1)}, u32[]{:S(2)}, u32[]{:S(2)}) collective-permute-start(bf16[1,8,4,32,128]{4,3,2,1,0:T(8,128)(2,1)S(1)} %bitcast.31), channel_id=1, source_target_pairs={{0,16},{8,24},{16,0},{24,8},{1,17},{9,25},{17,1},{25,9},{2,18},{10... | collective-permute-start | bytes 786440 | tf_op jit(solution)/shard_map/ppermute | solution.py:21
  93.8 26.9 %collective-permute-start.7 = (bf16[2,128,1024]{2,1,0:T(8,128)(2,1)}, bf16[2,128,1024]{2,1,0:T(8,128)(2,1)}, u32[]{:S(2)}, u32[]{:S(2)}) collective-permute-start(bf16[2,128,1024]{2,1,0:T(8,128)(2,1)} %collective-permute-done.6), channel_id=1, source_target_pairs={{0,1},{1,0},{2,3},{3,2},{4,5},{5,4},{6,7},{7,6},{8,9},{9,8},{10,11... | collective-permute-start | bytes 1572872 | tf_op jit(solution)/shard_map/ppermute | solution.py:21
  95.4 25.7 %collective-permute-start.8 = (bf16[2,128,1024]{2,1,0:T(8,128)(2,1)}, bf16[2,128,1024]{2,1,0:T(8,128)(2,1)}, u32[]{:S(2)}, u32[]{:S(2)}) collective-permute-start(bf16[2,128,1024]{2,1,0:T(8,128)(2,1)} %collective-permute-done.5.refs_0_), channel_id=1, source_target_pairs={{0,16},{8,24},{16,0},{24,8},{1,17},{9,25},{17,1},{25,9},{2,18},{10... | collective-permute-start | bytes 1572872 | tf_op jit(solution)/shard_map/ppermute | solution.py:21
  98.2 36.7 %copy-start.2 = (bf16[4,128,1024]{2,1,0:T(8,128)(2,1)}, bf16[4,128,1024]{2,1,0:T(8,128)(2,1)S(1)}, u32[]{:S(2)}) copy-start(bf16[4,128,1024]{2,1,0:T(8,128)(2,1)S(1)} %pad_maximum_fusion.1.refs_0_) | copy-start | bytes 3145732
  108.0 2.6 %copy-start.12 = (bf16[512,512]{1,0:T(8,128)(2,1)}, bf16[512,512]{1,0:T(8,128)(2,1)S(1)}, u32[]{:S(2)}) copy-start(bf16[512,512]{1,0:T(8,128)(2,1)S(1)} %collective-permute-done.24.refs_4_) | copy-start | bytes 1572868
  108.0 52.9 %collective-permute-start.14 = (bf16[4,128,1024]{2,1,0:T(8,128)(2,1)S(1)}, bf16[4,128,1024]{2,1,0:T(8,128)(2,1)}, u32[]{:S(2)}, u32[]{:S(2)}) collective-permute-start(bf16[4,128,1024]{2,1,0:T(8,128)(2,1)S(1)} %pad_maximum_fusion.1.refs_0_), channel_id=1, source_target_pairs={{0,16},{8,24},{16,0},{24,8},{1,17},{9,25},{17,1},{25,9},{2,18},{10... | collective-permute-start | bytes 3145736 | tf_op jit(solution)/shard_map/ppermute | solution.py:21
  108.6 16.0 %collective-permute-start.19 = (bf16[2,128,1024]{2,1,0:T(8,128)(2,1)}, bf16[2,128,1024]{2,1,0:T(8,128)(2,1)}, u32[]{:S(2)}, u32[]{:S(2)}) collective-permute-start(bf16[2,128,1024]{2,1,0:T(8,128)(2,1)} %get-tuple-element.25), channel_id=1, source_target_pairs={{0,2},{1,3},{2,0},{3,1},{4,6},{5,7},{6,4},{7,5},{8,10},{9,11},{10,... | collective-permute-start | bytes 1572872 | tf_op jit(solution)/shard_map/ppermute | solution.py:21
  109.0 6.6 %copy-start.7 = (bf16[1,8,4,32,128]{4,3,2,1,0:T(8,128)(2,1)}, bf16[1,8,4,32,128]{4,3,2,1,0:T(8,128)(2,1)S(1)}, u32[]{:S(2)}) copy-start(bf16[1,8,4,32,128]{4,3,2,1,0:T(8,128)(2,1)S(1)} %collective-permute-done.2) | copy-start | bytes 786436
  109.0 25.9 %collective-permute-start.22 = (bf16[2,128,1024]{2,1,0:T(8,128)(2,1)}, bf16[2,128,1024]{2,1,0:T(8,128)(2,1)}, u32[]{:S(2)}, u32[]{:S(2)}) collective-permute-start(bf16[2,128,1024]{2,1,0:T(8,128)(2,1)} %get-tuple-element.28), channel_id=1, source_target_pairs={{0,2},{1,3},{2,0},{3,1},{4,6},{5,7},{6,4},{7,5},{8,10},{9,11},{10,... | collective-permute-start | bytes 1572872 | tf_op jit(solution)/shard_map/ppermute | solution.py:21
  115.6 19.4 %copy-start.3 = (f32[2,128,1024]{2,1,0:T(8,128)S(1)}, f32[2,128,1024]{2,1,0:T(8,128)}, u32[]{:S(2)}) copy-start(f32[2,128,1024]{2,1,0:T(8,128)} %get-tuple-element.24.refs_0_) | copy-start | bytes 3145732
  120.7 15.5 %copy-start.4 = (f32[2,128,1024]{2,1,0:T(8,128)S(1)}, f32[2,128,1024]{2,1,0:T(8,128)}, u32[]{:S(2)}) copy-start(f32[2,128,1024]{2,1,0:T(8,128)} %get-tuple-element.27.refs_0_) | copy-start | bytes 3145732
  120.7 28.3 %collective-permute-start.25 = (bf16[2,128,1024]{2,1,0:T(8,128)(2,1)}, bf16[2,128,1024]{2,1,0:T(8,128)(2,1)}, u32[]{:S(2)}, u32[]{:S(2)}) collective-permute-start(bf16[2,128,1024]{2,1,0:T(8,128)(2,1)} %get-tuple-element.31), channel_id=1, source_target_pairs={{0,2},{1,3},{2,0},{3,1},{4,6},{5,7},{6,4},{7,5},{8,10},{9,11},{10,... | collective-permute-start | bytes 1572872 | tf_op jit(solution)/shard_map/ppermute | solution.py:21
  121.1 39.7 %collective-permute-start.28 = (bf16[2,128,1024]{2,1,0:T(8,128)(2,1)}, bf16[2,128,1024]{2,1,0:T(8,128)(2,1)}, u32[]{:S(2)}, u32[]{:S(2)}) collective-permute-start(bf16[2,128,1024]{2,1,0:T(8,128)(2,1)} %get-tuple-element.34), channel_id=1, source_target_pairs={{0,2},{1,3},{2,0},{3,1},{4,6},{5,7},{6,4},{7,5},{8,10},{9,11},{10,... | collective-permute-start | bytes 1572872 | tf_op jit(solution)/shard_map/ppermute | solution.py:21
  124.6 36.3 %collective-permute-start.3 = (bf16[2,8,4,32,128]{4,3,2,1,0:T(8,128)(2,1)}, bf16[2,8,4,32,128]{4,3,2,1,0:T(8,128)(2,1)}, u32[]{:S(2)}, u32[]{:S(2)}) collective-permute-start(bf16[2,8,4,32,128]{4,3,2,1,0:T(8,128)(2,1)} %pad_maximum_fusion.2), channel_id=1, source_target_pairs={{0,8},{8,0},{16,24},{24,16},{1,9},{9,1},{17,25},{25,17},{2,10},{10... | collective-permute-start | bytes 1572872 | tf_op jit(solution)/shard_map/ppermute | solution.py:21
  134.9 61.0 %collective-permute-start.15 = (bf16[4,128,1024]{2,1,0:T(8,128)(2,1)S(1)}, bf16[4,128,1024]{2,1,0:T(8,128)(2,1)}, u32[]{:S(2)}, u32[]{:S(2)}) collective-permute-start(bf16[4,128,1024]{2,1,0:T(8,128)(2,1)S(1)} %pad_maximum_fusion.1.refs_0_), channel_id=1, source_target_pairs={{0,8},{8,0},{16,24},{24,16},{1,9},{9,1},{17,25},{25,17},{2,10},{10... | collective-permute-start | bytes 3145736 | tf_op jit(solution)/shard_map/ppermute | solution.py:21
  134.9 27.5 %copy-start.5 = (f32[2,128,1024]{2,1,0:T(8,128)S(1)}, f32[2,128,1024]{2,1,0:T(8,128)}, u32[]{:S(2)}) copy-start(f32[2,128,1024]{2,1,0:T(8,128)} %get-tuple-element.30.refs_3_) | copy-start | bytes 3145732
  134.9 28.6 %copy-start.6 = (f32[2,128,1024]{2,1,0:T(8,128)S(1)}, f32[2,128,1024]{2,1,0:T(8,128)}, u32[]{:S(2)}) copy-start(f32[2,128,1024]{2,1,0:T(8,128)} %get-tuple-element.33.refs_0_) | copy-start | bytes 3145732
  136.1 62.8 %copy-start.8 = (bf16[1,8,4,32,128]{4,3,2,1,0:T(8,128)(2,1)S(1)}, bf16[1,8,4,32,128]{4,3,2,1,0:T(8,128)(2,1)}, u32[]{:S(2)}) copy-start(bf16[1,8,4,32,128]{4,3,2,1,0:T(8,128)(2,1)} %copy-done.7) | copy-start | bytes 786436
  149.0 15.6 %collective-permute-start.20 = (bf16[1,128,1024]{2,1,0:T(8,128)(2,1)S(1)}, bf16[1,128,1024]{2,1,0:T(8,128)(2,1)S(1)}, u32[]{:S(2)}, u32[]{:S(2)}) collective-permute-start(bf16[1,128,1024]{2,1,0:T(8,128)(2,1)S(1)} %fusion.3), channel_id=1, source_target_pairs={{0,4},{1,5},{2,6},{3,7},{4,0},{5,1},{6,2},{7,3},{8,12},{9,13},{10,... | collective-permute-start | bytes 786440 | tf_op jit(solution)/shard_map/ppermute | solution.py:21
  160.9 17.7 %collective-permute-start.23 = (bf16[1,128,1024]{2,1,0:T(8,128)(2,1)S(1)}, bf16[1,128,1024]{2,1,0:T(8,128)(2,1)S(1)}, u32[]{:S(2)}, u32[]{:S(2)}) collective-permute-start(bf16[1,128,1024]{2,1,0:T(8,128)(2,1)S(1)} %fusion.2), channel_id=1, source_target_pairs={{0,4},{1,5},{2,6},{3,7},{4,0},{5,1},{6,2},{7,3},{8,12},{9,13},{10,... | collective-permute-start | bytes 786440 | tf_op jit(solution)/shard_map/ppermute | solution.py:21
  160.9 50.1 %collective-permute-start.16 = (bf16[4,128,1024]{2,1,0:T(8,128)(2,1)}, bf16[4,128,1024]{2,1,0:T(8,128)(2,1)S(1)}, u32[]{:S(2)}, u32[]{:S(2)}) collective-permute-start(bf16[4,128,1024]{2,1,0:T(8,128)(2,1)} %collective-permute-done.14.refs_1_), channel_id=1, source_target_pairs={{0,8},{8,0},{16,24},{24,16},{1,9},{9,1},{17,25},{25,17},{2,10},{10... | collective-permute-start | bytes 3145736 | tf_op jit(solution)/shard_map/ppermute | solution.py:21
  160.9 34.6 %collective-permute-start.9 = (bf16[2,128,1024]{2,1,0:T(8,128)(2,1)}, bf16[2,128,1024]{2,1,0:T(8,128)(2,1)S(1)}, u32[]{:S(2)}, u32[]{:S(2)}) collective-permute-start(bf16[2,128,1024]{2,1,0:T(8,128)(2,1)} %collective-permute-done.7.refs_1_), channel_id=1, source_target_pairs={{0,16},{8,24},{16,0},{24,8},{1,17},{9,25},{17,1},{25,9},{2,18},{10... | collective-permute-start | bytes 1572872 | tf_op jit(solution)/shard_map/ppermute | solution.py:21
  164.5 39.6 %copy-start.14 = (bf16[1,128,1024]{2,1,0:T(8,128)(2,1)}, bf16[1,128,1024]{2,1,0:T(8,128)(2,1)S(1)}, u32[]{:S(2)}) copy-start(bf16[1,128,1024]{2,1,0:T(8,128)(2,1)S(1)} %collective-permute-done.20.refs_2_) | copy-start | bytes 786436
  164.6 25.3 %collective-permute-start.26 = (bf16[1,128,1024]{2,1,0:T(8,128)(2,1)S(1)}, bf16[1,128,1024]{2,1,0:T(8,128)(2,1)S(1)}, u32[]{:S(2)}, u32[]{:S(2)}) collective-permute-start(bf16[1,128,1024]{2,1,0:T(8,128)(2,1)S(1)} %fusion.1), channel_id=1, source_target_pairs={{0,4},{1,5},{2,6},{3,7},{4,0},{5,1},{6,2},{7,3},{8,12},{9,13},{10,... | collective-permute-start | bytes 786440 | tf_op jit(solution)/shard_map/ppermute | solution.py:21
  178.6 17.3 %copy-start.15 = (bf16[1,128,1024]{2,1,0:T(8,128)(2,1)}, bf16[1,128,1024]{2,1,0:T(8,128)(2,1)S(1)}, u32[]{:S(2)}) copy-start(bf16[1,128,1024]{2,1,0:T(8,128)(2,1)S(1)} %collective-permute-done.23.refs_2_) | copy-start | bytes 786436
  178.6 16.8 %collective-permute-start.29 = (bf16[1,128,1024]{2,1,0:T(8,128)(2,1)S(1)}, bf16[1,128,1024]{2,1,0:T(8,128)(2,1)S(1)}, u32[]{:S(2)}, u32[]{:S(2)}) collective-permute-start(bf16[1,128,1024]{2,1,0:T(8,128)(2,1)S(1)} %fusion), channel_id=1, source_target_pairs={{0,4},{1,5},{2,6},{3,7},{4,0},{5,1},{6,2},{7,3},{8,12},{9,13},{10,... | collective-permute-start | bytes 786440 | tf_op jit(solution)/shard_map/ppermute | solution.py:21
  189.8 6.1 %copy-start.16 = (bf16[1,128,1024]{2,1,0:T(8,128)(2,1)}, bf16[1,128,1024]{2,1,0:T(8,128)(2,1)S(1)}, u32[]{:S(2)}) copy-start(bf16[1,128,1024]{2,1,0:T(8,128)(2,1)S(1)} %collective-permute-done.26.refs_5_) | copy-start | bytes 786436
  189.8 30.5 %collective-permute-start.10 = (bf16[2,128,1024]{2,1,0:T(8,128)(2,1)}, bf16[2,128,1024]{2,1,0:T(8,128)(2,1)}, u32[]{:S(2)}, u32[]{:S(2)}) collective-permute-start(bf16[2,128,1024]{2,1,0:T(8,128)(2,1)} %collective-permute-done.5.refs_0_), channel_id=1, source_target_pairs={{0,8},{8,0},{16,24},{24,16},{1,9},{9,1},{17,25},{25,17},{2,10},{10... | collective-permute-start | bytes 1572872 | tf_op jit(solution)/shard_map/ppermute | solution.py:21
  195.4 24.9 %collective-permute-start.11 = (bf16[2,128,1024]{2,1,0:T(8,128)(2,1)}, bf16[2,128,1024]{2,1,0:T(8,128)(2,1)}, u32[]{:S(2)}, u32[]{:S(2)}) collective-permute-start(bf16[2,128,1024]{2,1,0:T(8,128)(2,1)} %collective-permute-done.7.refs_1_), channel_id=1, source_target_pairs={{0,8},{8,0},{16,24},{24,16},{1,9},{9,1},{17,25},{25,17},{2,10},{10... | collective-permute-start | bytes 1572872 | tf_op jit(solution)/shard_map/ppermute | solution.py:21
  195.5 8.6 %copy-start.10 = (bf16[2,128,1024]{2,1,0:T(8,128)(2,1)}, bf16[2,128,1024]{2,1,0:T(8,128)(2,1)S(1)}, u32[]{:S(2)}) copy-start(bf16[2,128,1024]{2,1,0:T(8,128)(2,1)S(1)} %collective-permute-done.9.refs_3_) | copy-start | bytes 1572868
  195.5 24.8 %collective-permute-start.12 = (bf16[2,128,1024]{2,1,0:T(8,128)(2,1)}, bf16[2,128,1024]{2,1,0:T(8,128)(2,1)}, u32[]{:S(2)}, u32[]{:S(2)}) collective-permute-start(bf16[2,128,1024]{2,1,0:T(8,128)(2,1)} %collective-permute-done.8.refs_2_), channel_id=1, source_target_pairs={{0,8},{8,0},{16,24},{24,16},{1,9},{9,1},{17,25},{25,17},{2,10},{10... | collective-permute-start | bytes 1572872 | tf_op jit(solution)/shard_map/ppermute | solution.py:21
  196.1 24.2 %collective-permute-start.13 = (bf16[2,128,1024]{2,1,0:T(8,128)(2,1)S(1)}, bf16[2,128,1024]{2,1,0:T(8,128)(2,1)S(1)}, u32[]{:S(2)}, u32[]{:S(2)}) collective-permute-start(bf16[2,128,1024]{2,1,0:T(8,128)(2,1)S(1)} %collective-permute-done.9.refs_3_), channel_id=1, source_target_pairs={{0,8},{8,0},{16,24},{24,16},{1,9},{9,1},{17,25},{25,17},{2,10},{10... | collective-permute-start | bytes 1572872 | tf_op jit(solution)/shard_map/ppermute | solution.py:21
  (4 other events, 4.6 us)
